TPU v7x, 128 devices: a whole 4x4x4 slice. The times are simulated.
128 devices in a mesh: blk: 32 (over z, y, x_hi), tp: 4 (over x_lo, core).
Axes of the slice: x: 4 (x_hi: 2, x_lo: 2; x = x_hi * 2 + x_lo), y: 4, z: 4, core: 2. Of those that a mesh axis runs over, the one named last changes fastest.
Arguments:
- tokens: bfloat16 [8192, 2048], P('blk'), may hold values from -27 to 27
- order: int32 [64], replicated, may hold values from 0 to 63, each once
- gain_attn: float32 [2048], replicated, may hold values from 0.1 to 1.9
- gain_ffn: float32 [2048], replicated, may hold values from 0.1 to 1.9
- w_query: bfloat16 [2048, 2048], P(None, 'tp'), may hold values from -3.7565048 to 3.7565048
- w_key: bfloat16 [2048, 512], P(None, 'tp'), may hold values from -0.13258252 to 0.13258252
- w_value: bfloat16 [2048, 512], P(None, 'tp'), may hold values from -0.125 to 0.125
- w_out: bfloat16 [2048, 2048], P('tp'), may hold values from -0.125 to 0.125
- w_gate: bfloat16 [2048, 8192], P(None, 'tp'), may hold values from -0.125 to 0.125
- w_up: bfloat16 [2048, 8192], P(None, 'tp'), may hold values from -0.125 to 0.125
- w_down: bfloat16 [8192, 2048], P('tp'), may hold values from -0.0625 to 0.0625
Outputs:
- layer_out: bfloat16 [8192, 2048], P('blk', 'tp')
Inputs may be any that keep to these rules, and one draw needn't show every extreme that they name: `order`: every number 0 to 63 appears once; device b of blk holds stored blocks 2b and 2b + 1.
All inputs are finite; a program needn't handle non-finite values.
Results may differ from a plain program's by a relative error of at most 0.0095.
Values may be sent and summed in bfloat16 or wider, within the bound.
A program may use at most 128 MiB of HBM per device.

v0:
```python
import jax
import jax.numpy as jnp
from jax import lax
from jax.sharding import PartitionSpec as P

HD = 64


EPS = 1e-05
ROPE_BASE = 500000.0
MASKED = -1e30


def gathered_total(shard, axis):
    return lax.all_gather(shard, axis).astype(jnp.float32).sum(0)


def in_blocks(shard, dim, peers):
    before, after = (shard.shape[:dim], shard.shape[dim + 1 :])
    return jnp.moveaxis(shard.reshape(*before, peers, -1, *after), dim, 0)


def sum_at_owner(shard, axis, dim):
    peers = lax.axis_size(axis)
    parts = lax.all_to_all(in_blocks(shard, dim, peers), axis, 0, 0, tiled=True)
    return jnp.sum(parts.astype(jnp.float32), axis=0)


def rotate(values, positions):
    half_dim = values.shape[-1] // 2
    freq = ROPE_BASE ** (-(jnp.arange(half_dim, dtype=jnp.float32) * 2.0 / values.shape[-1]))
    angle = positions.astype(jnp.float32)[:, None] * freq[None, :]
    cosine = jnp.cos(angle)[:, None, :]
    sine = jnp.sin(angle)[:, None, :]
    first = values[..., :half_dim]
    second = values[..., half_dim:]
    return jnp.concatenate(
        [first * cosine - second * sine, second * cosine + first * sine], axis=-1
    )


def stored_positions(order, start, count, half_rows):
    stored = start + jnp.arange(count, dtype=jnp.int32)
    which = stored // half_rows
    match = which[:, None] == jnp.arange(order.shape[0], dtype=jnp.int32)[None, :]
    first = jnp.sum(jnp.where(match, order[None, :], 0), axis=1)
    return first * half_rows + stored % half_rows


def local(tokens, order, gain_attn, gain_ffn, w_query, w_key, w_value, w_out, w_gate, w_up, w_down):
    tok_rows, model_width = tokens.shape
    half_rows = tok_rows // 2
    kv_local = w_key.shape[1] // HD
    query_local = w_query.shape[1] // HD
    group = query_local // kv_local
    score_scale = HD ** (-0.5)
    query_pos = stored_positions(order, lax.axis_index("blk") * tok_rows, tok_rows, half_rows)
    tokens_wide = tokens.astype(jnp.float32)
    normed = (
        tokens_wide
        * lax.rsqrt(jnp.mean(tokens_wide * tokens_wide, axis=-1, keepdims=True) + EPS)
        * gain_attn
    ).astype(jnp.bfloat16)
    queries = jnp.dot(normed, w_query, preferred_element_type=jnp.float32).reshape(
        tok_rows, query_local, HD
    )
    queries = rotate(queries, query_pos).astype(jnp.bfloat16).reshape(tok_rows, kv_local, group, HD)
    keys = jnp.dot(normed, w_key, preferred_element_type=jnp.float32).reshape(
        tok_rows, kv_local, HD
    )
    keys = rotate(keys, query_pos).astype(jnp.bfloat16)
    values = jnp.dot(normed, w_value, preferred_element_type=jnp.float32).astype(jnp.bfloat16)
    packed = jnp.concatenate([keys.reshape(tok_rows, kv_local * HD), values], axis=1)

    def attend(carry, block, key_pos):
        running, denominator, accum = carry
        key_block = block[:, : kv_local * HD].reshape(-1, kv_local, HD)
        value_block = block[:, kv_local * HD :].reshape(-1, kv_local, HD)
        scores = (
            jnp.einsum("qkgd,skd->kgqs", queries, key_block, preferred_element_type=jnp.float32)
            * score_scale
        )
        allowed = key_pos[None, :] <= query_pos[:, None]
        scores = jnp.where(allowed, scores, MASKED)
        newest = jnp.maximum(running, jnp.max(scores, axis=-1))
        weights = jnp.where(allowed, jnp.exp(scores - newest[..., None]), 0.0)
        factor = jnp.exp(running - newest)
        denominator = denominator * factor + jnp.sum(weights, axis=-1)
        accum = accum * factor[..., None] + jnp.einsum(
            "kgqs,skd->kgqd",
            weights.astype(jnp.bfloat16),
            value_block,
            preferred_element_type=jnp.float32,
        )
        return (newest, denominator, accum)

    def consider(carry, block, key_pos):
        return attend(carry, block, key_pos)

    start_carry = (
        jnp.full((kv_local, group, tok_rows), MASKED, jnp.float32),
        jnp.zeros((kv_local, group, tok_rows), jnp.float32),
        jnp.zeros((kv_local, group, tok_rows, HD), jnp.float32),
    )
    piece = lax.all_gather(packed, "blk", axis=0, tiled=True)
    count = piece.shape[0]
    key_pos = stored_positions(order, jnp.int32(0), count, half_rows)
    turns = min(16, count // 512)
    size = count // turns

    def one_turn(turn, inner):
        offset = turn * size
        return consider(
            inner,
            lax.dynamic_slice_in_dim(piece, offset, size, 0),
            lax.dynamic_slice_in_dim(key_pos, offset, size, 0),
        )

    running, denominator, accum = lax.fori_loop(0, turns, one_turn, start_carry)
    heads = (accum / denominator[..., None]).astype(jnp.bfloat16)
    heads = jnp.transpose(heads, (2, 0, 1, 3)).reshape(tok_rows, query_local * HD)
    partial_value = jnp.dot(heads, w_out, preferred_element_type=jnp.float32)
    share = model_width // lax.axis_size("tp")
    col_start = lax.axis_index("tp") * share
    attention = gathered_total(partial_value.astype(jnp.bfloat16), "tp").astype(jnp.float32)
    resid_full = tokens_wide + attention
    normed_ffn = (
        resid_full
        * lax.rsqrt(jnp.mean(resid_full * resid_full, axis=-1, keepdims=True) + EPS)
        * gain_ffn
    ).astype(jnp.bfloat16)
    gate = jnp.dot(normed_ffn, w_gate, preferred_element_type=jnp.float32)
    up_proj = jnp.dot(normed_ffn, w_up, preferred_element_type=jnp.float32)
    residual = lax.dynamic_slice_in_dim(resid_full, col_start, share, 1)
    hidden = (jax.nn.silu(gate) * up_proj).astype(jnp.bfloat16)
    down = jnp.dot(hidden, w_down, preferred_element_type=jnp.float32)
    feed = sum_at_owner(down.astype(jnp.bfloat16), "tp", 1)
    return (residual + feed).astype(jnp.bfloat16)


def solution(mesh):
    placed = (
        P("blk", None),
        P(),
        P(),
        P(),
        P(None, "tp"),
        P(None, "tp"),
        P(None, "tp"),
        P("tp", None),
        P(None, "tp"),
        P(None, "tp"),
        P("tp", None),
    )
    return jax.shard_map(
        local, mesh=mesh, in_specs=placed, out_specs=P("blk", "tp"), check_vma=False
    )
```

profile of v0, /device:TPU:1, one launch (start us, length us, event | category | flops | bytes accessed | tf_op | source)
XLA Modules:
  0.0 275.2 jit_solution(524990952638176915)
XLA Ops:
  6.6 1.7 fusion.14
  9.1 1.9 convolution_convert_fusion.2
  12.7 2.6 fusion.29
  15.9 75.9 %all-gather.4.cloned.1.call-done = bf16[8192,256]{0,1:T(8,128)(2,1)} async-done(((bf16[256,256]{0,1:T(8,128)(2,1)}), bf16[8192,256]{0,1:T(8,128)(2,1)}) %all-gather.4.cloned.1.call-update) | async-done | bytes 4194320 | tf_op jit(solution)/shard_map/all_gather | solution.py:105
  91.8 82.9 %while.18 = (s32[]{:T(128)}, f32[2,4,256]{2,1,0:T(4,128)S(1)}, f32[2,4,256]{2,1,0:T(4,128)S(1)}, f32[2,4,256,64]{2,3,1,0:T(8,128)}, s32[8192]{0:T(1024)S(1)}, /*...) while((s32[]{:T(128)}, f32[2,4,256]{2,1,0:T(4,128)S(1)}, ...), condition=%wide.region_6.7_spmd.clone, body=%wide.region_3.6_spmd.clone.sunk | while | flops 282601472 | bytes 19537168 | solution.py:119
  94.9 1.3 fusion.65
  100.1 1.3 fusion.65
  110.4 1.3 fusion.65
  115.6 1.3 fusion.65
  126.0 1.3 fusion.65
  131.1 1.3 fusion.65
  141.5 1.3 fusion.65
  146.7 1.3 fusion.65
  151.9 1.3 fusion.65
  157.0 1.3 fusion.65
  175.7 1.7 convolution_convert_fusion
  177.5 47.5 %all-gather.6.cloned.1.call-done = bf16[1024,2048]{1,0:T(8,128)(2,1)} async-done(((bf16[256,2048]{1,0:T(8,128)(2,1)}), bf16[1024,2048]{1,0:T(8,128)(2,1)}) %all-gather.6.cloned.1.call-update) | async-done | bytes 4194320 | tf_op jit(solution)/shard_map/all_gather | solution.py:15
  225.0 3.3 %convert_reduce_fusion = f32[256,2048]{1,0:T(8,128)S(1)} fusion(bf16[4,256,2048]{2,1,0:T(8,128)(2,1)} %bitcast.68), kind=kLoop, calls=%fused_computation.18 | loop fusion | flops 3670016 | bytes 6291456 | tf_op jit(solution)/shard_map/reduce_sum | solution.py:15
  228.7 1.3 copy-done.2
  230.0 7.1 %fusion.28 = f32[256,2048]{1,0:T(8,128)} fusion(bf16[2048,2048]{1,0:T(8,128)(2,1)} %param.21, f32[256,2048]{1,0:T(8,128)S(1)} %get-tuple-element.193, f32[2048]{0:T(1024)S(1)} %copy-done.8, f32[256]{0:T(256)S(1)} %add_rsqrt_fusion), kind=kOutput, calls=%fused_computation.74 | convolution fusion | flops 2149056512 | bytes 12592128 | tf_op jit(solution)/shard_map/dot_general | solution.py:132
  237.1 11.7 %convolution_convert_fusion.1 = bf16[256,2048]{1,0:T(8,128)(2,1)S(1)} fusion(bf16[2048,2048]{1,0:T(8,128)(2,1)} %param.23, bf16[2048,2048]{1,0:T(8,128)(2,1)} %param.22, f32[256,2048]{1,0:T(8,128)} %fusion.28, f32[256,2048]{1,0:T(8,128)} %copy-done.2, f32[2048]{0:T(1024)S(1)} %copy-done.8, f32[256]{0:T(256)S(1)} %add_rsqrt_fusion), kind=kOutput, calls=%fused_computation.25 | convolution fusion | flops 4300210176 | bytes 22029312 | tf_op jit(solution)/shard_map/dot_general | solution.py:136
  249.9 3.5 %all-to-all-start = ((bf16[4,256,512]{2,1,0:T(8,128)(2,1)}), bf16[4,256,512]{2,1,0:T(8,128)(2,1)S(1)}, u32[]{:S(2)}, u32[]{:S(2)}) async-start(bf16[4,256,512]{2,1,0:T(8,128)(2,1)} %bitcast.69), calls=%async_computation | async-start | bytes 2097152 | tf_op jit(solution)/shard_map/all_to_all | solution.py:25
  253.4 13.0 %all-to-all-done = bf16[4,256,512]{2,1,0:T(8,128)(2,1)S(1)} async-done(((bf16[4,256,512]{2,1,0:T(8,128)(2,1)}), bf16[4,256,512]{2,1,0:T(8,128)(2,1)S(1)}, u32[]{:S(2)}, u32[]{:S(2)}) %all-to-all-start) | async-done | bytes 1048608 | tf_op jit(solution)/shard_map/all_to_all | solution.py:25
  266.5 1.8 add_convert_fusion
  (238 shorter events, 74.8 us)
Async XLA Ops:
  6.5 169.2 %copy-start = (bf16[512,2048]{1,0:T(8,128)(2,1)S(1)}, bf16[512,2048]{1,0:T(8,128)(2,1)}, u32[]{:S(2)}) copy-start(bf16[512,2048]{1,0:T(8,128)(2,1)} %param.20) | copy-start | bytes 6291460
  6.5 4.5 %copy-start.1 = (bf16[256,2048]{1,0:T(8,128)(2,1)S(1)}, bf16[256,2048]{1,0:T(8,128)(2,1)}, u32[]{:S(2)}) copy-start(bf16[256,2048]{1,0:T(8,128)(2,1)} %param.13) | copy-start | bytes 3145732
  6.5 4.5 %copy-start.7 = (f32[2048]{0:T(1024)S(1)}, f32[2048]{0:T(1024)}, u32[]{:S(2)}) copy-start(f32[2048]{0:T(1024)} %param.15) | copy-start | bytes 24580
  6.5 85.2 %all-gather.4.cloned.1.call-start = ((), (), s32[]{:S(2)}) async-start(), calls=%async_computation.1 | async-start | bytes 4325376 | tf_op jit(solution)/shard_map/all_gather | solution.py:105
  8.2 2.8 %copy-start.6 = (bf16[2048,128]{1,0:T(8,128)(2,1)S(1)}, bf16[2048,128]{1,0:T(8,128)(2,1)}, u32[]{:S(2)}) copy-start(bf16[2048,128]{1,0:T(8,128)(2,1)} %param.18) | copy-start | bytes 1572868
  12.6 212.4 %all-gather.6.cloned.1.call-start = ((), (), s32[]{:S(2)}) async-start(), calls=%async_computation.2 | async-start | bytes 5242880 | tf_op jit(solution)/shard_map/all_gather | solution.py:15
  12.7 2.7 copy-start.5
  93.8 1.0 copy-start.3
  99.0 1.0 copy-start.3
  104.2 1.0 copy-start.3
  109.4 1.0 copy-start.3
  114.5 1.0 copy-start.3
  119.7 1.0 copy-start.3
  124.9 1.0 copy-start.3
  130.1 1.0 copy-start.3
  135.3 1.0 copy-start.3
  140.4 1.0 copy-start.3
  145.6 1.0 copy-start.3
  150.8 1.0 copy-start.3
  161.2 1.0 copy-start.3
  171.5 1.0 copy-start.3
  228.3 1.7 copy-start.8
  228.7 1.3 copy-start.2
  249.9 16.5 %all-to-all-start = ((bf16[4,256,512]{2,1,0:T(8,128)(2,1)}), bf16[4,256,512]{2,1,0:T(8,128)(2,1)S(1)}, u32[]{:S(2)}, u32[]{:S(2)}) async-start(bf16[4,256,512]{2,1,0:T(8,128)(2,1)} %bitcast.69), calls=%async_computation | async-start | bytes 2097152 | tf_op jit(solution)/shard_map/all_to_all | solution.py:25
  (18 other events, 14.7 us)
Sparse Core Ops, SparseCore 0:
  12.7 79.0 all-gather.3
  177.6 47.3 all-gather.5
where the time goes:
time: 277 us; the launch traced here: 275 us
  waiting for transfers between devices  136 us (49%)
  matrix products  59 us (21%)
  local copies, waits for them, and re-layouts  32 us (12%)
  other arithmetic  29.5 us (11%)
  between operations  13.6 us (5%)
  starting transfers between devices  3.55 us (1%)
    all_gather x1, waiting for transfers between devices, local(): piece = lax.all_gather(packed, 'blk', axis=0, tiled=True)  75.9 us
    all_gather x1, waiting for transfers between devices, gathered_total(): return lax.all_gather(shard, axis).astype(jnp.float32).sum(0)  47.5 us
    dot_general x16, matrix products, attend(): jnp.einsum('kgqs,skd->kgqd', weights.astype(jnp.bfloat16), value_block, p...  20.3 us
    reduce_sum x16, other arithmetic, attend(): denominator = denominator * factor + jnp.sum(weights, axis=-1)  16.1 us
    slice x16, local copies, waits for them, and re-layouts, attend(): value_block = block[:, kv_local * HD:].reshape(-1, kv_local, HD)  15.9 us
    dot_general x16, matrix products, attend(): jnp.einsum('qkgd,skd->kgqs', queries, key_block, preferred_element_type=j...  13.1 us
    all_to_all x1, waiting for transfers between devices, sum_at_owner(): parts = lax.all_to_all(in_blocks(shard, dim, peers), axis, 0, 0, tiled=True)  13 us
    while x80, local copies, waits for them, and re-layouts  12.5 us
  transfers between devices with their start and end apart: 3, of which 3 were waited for; matrix products, arithmetic and copies ran while one was open for 1% of the time, Pallas kernels for 0%

commit v1 on v0

v1 whole, which is shorter than its diff:
```python
import functools

import jax
import jax.numpy as jnp
from jax import lax
from jax.experimental import pallas as pl
from jax.experimental.pallas import tpu as pltpu
from jax.sharding import PartitionSpec as P

HD = 64
EPS = 1e-05
ROPE_BASE = 500000.0
BIG = 1e30
LOG2E = 1.4426950408889634
MESH = pl.DeviceIdType.MESH


def gathered_total(shard, axis):
    return lax.all_gather(shard, axis).astype(jnp.float32).sum(0)


def in_blocks(shard, dim, peers):
    before, after = (shard.shape[:dim], shard.shape[dim + 1 :])
    return jnp.moveaxis(shard.reshape(*before, peers, -1, *after), dim, 0)


def sum_at_owner(shard, axis, dim):
    peers = lax.axis_size(axis)
    parts = lax.all_to_all(in_blocks(shard, dim, peers), axis, 0, 0, tiled=True)
    return jnp.sum(parts.astype(jnp.float32), axis=0)


def origin(flow, major, minor, x):
    if flow == 0:
        return minor * 8 + major * 2 + x
    return major * 8 + minor * 2 + x


def plane(i, major, x):
    k = i // 2
    step = (3 * k + 3 * (k // 2) + 2 * (k // 3)) % 4
    return (major + step) % 4, (x + i) % 2


def attention_kernel(
    tok, gain, wq, wk, wv, cos, sin, bias, diag, out,
    normed, kv, qp, m_ref, l_ref, acc, send_sem, recv_sem,
):
    b = lax.axis_index("blk")
    z, y, x = b // 8, (b // 2) % 4, b % 2
    coords = ((y, z), (z, y))

    barrier = pltpu.get_barrier_semaphore()
    peers = [origin(0, y, z, (x + 1) % 2)]
    peers += [origin(0, (y + d) % 4, z, x) for d in (1, 3)]
    peers += [origin(0, y, (z + d) % 4, x) for d in (1, 3)]
    for peer in peers:
        pl.semaphore_signal(barrier, inc=1, device_id={"blk": peer}, device_id_type=MESH)

    rows = 64

    def norm_rows(r, _):
        at = pl.ds(pl.multiple_of(r * rows, rows), rows)
        t = tok[at, :].astype(jnp.float32)
        scale = lax.rsqrt(jnp.mean(t * t, axis=-1, keepdims=True) + EPS)
        normed[at, :] = (t * scale * gain[...]).astype(jnp.bfloat16)
        return 0

    lax.fori_loop(0, 256 // rows, norm_rows, 0)

    c = cos[...]
    s = sin[...]

    def rotated(u):
        a, h = u[0:32], u[32:64]
        return jnp.concatenate([a * c - h * s, h * c + a * s], axis=0)

    k = jnp.dot(normed[...], wk[...], preferred_element_type=jnp.float32).T
    kt = jnp.concatenate([rotated(k[0:64]), rotated(k[64:128])], axis=0)
    kn = kt.T.astype(jnp.bfloat16)
    v = jnp.dot(normed[...], wv[...], preferred_element_type=jnp.float32).T.astype(jnp.bfloat16)
    for f in range(2):
        kv[2 * b + f, 0:128, :] = kn[128 * f : 128 * f + 128, :]
        kv[2 * b + f, 128:256, :] = v[:, 128 * f : 128 * f + 128]

    pl.semaphore_wait(barrier, 5)

    def copy(f, org, dest, i, which):
        unit = 2 * org + f
        return pltpu.make_async_remote_copy(
            src_ref=kv.at[unit], dst_ref=kv.at[unit],
            send_sem=send_sem.at[f, i, which], recv_sem=recv_sem.at[unit],
            device_id={"blk": dest}, device_id_type=MESH,
        )

    def arrived(f, org):
        unit = 2 * org + f
        pltpu.make_async_remote_copy(
            src_ref=kv.at[unit], dst_ref=kv.at[unit],
            send_sem=send_sem.at[f, 0, 0], recv_sem=recv_sem.at[unit],
            device_id={"blk": peers[0]}, device_id_type=MESH,
        ).wait_recv()

    for f in range(2):
        major, minor = coords[f]
        copy(f, b, origin(f, major, minor, (x + 1) % 2), 0, 4).start()
    for f in range(2):
        major, minor = coords[f]
        copy(f, b, origin(f, (major + 1) % 4, minor, x), 0, 2).start()
        copy(f, b, origin(f, (major + 3) % 4, minor, x), 0, 3).start()
    for f in range(2):
        major, minor = coords[f]
        copy(f, b, origin(f, major, (minor + 1) % 4, x), 0, 0).start()
        copy(f, b, origin(f, major, (minor + 3) % 4, x), 0, 1).start()

    zero = jnp.zeros((64, 256), jnp.bfloat16)
    for half in range(2):
        q = jnp.dot(
            normed[...], wq[:, 256 * half : 256 * half + 256], preferred_element_type=jnp.float32
        ).T
        for n in range(4):
            u = (rotated(q[64 * n : 64 * n + 64]) * (HD**-0.5 * LOG2E)).astype(jnp.bfloat16)
            top, low = (u, zero) if half == 0 else (zero, u)
            qp[half, n, 0:64, :] = top
            qp[half, n, 64:128, :] = low

    def attend(ja, jb, first):
        ka, kb = kv[ja, 0:128, :], kv[jb, 0:128, :]
        if not first:
            ba, bb = bias[pl.ds(ja, 1), :], bias[pl.ds(jb, 1), :]
        for g in range(2):
            va = kv[ja, 128 + 64 * g : 192 + 64 * g, :]
            vb = kv[jb, 128 + 64 * g : 192 + 64 * g, :]
            vt = jnp.concatenate([va, vb], axis=1)
            for n in range(4):
                sa = jnp.dot(ka, qp[g, n], preferred_element_type=jnp.float32)
                sb = jnp.dot(kb, qp[g, n], preferred_element_type=jnp.float32)
                row = 4 * g + n
                if first:
                    sa = sa + diag[0:128, :]
                    sb = sb + diag[128:256, :]
                    new = jnp.maximum(
                        jnp.max(sa, axis=0, keepdims=True), jnp.max(sb, axis=0, keepdims=True)
                    )
                    pa, pb = jnp.exp2(sa - new), jnp.exp2(sb - new)
                else:
                    old = m_ref[row : row + 1, :]
                    new = jnp.maximum(
                        old,
                        jnp.maximum(
                            jnp.max(sa, axis=0, keepdims=True) - ba,
                            jnp.max(sb, axis=0, keepdims=True) - bb,
                        ),
                    )
                    pa, pb = jnp.exp2(sa - (new + ba)), jnp.exp2(sb - (new + bb))
                total = jnp.sum(pa, axis=0, keepdims=True) + jnp.sum(pb, axis=0, keepdims=True)
                p = jnp.concatenate([pa, pb], axis=0).astype(jnp.bfloat16)
                o = jnp.dot(vt, p, preferred_element_type=jnp.float32)
                if first:
                    l_ref[row : row + 1, :] = total
                    acc[64 * row : 64 * row + 64, :] = o
                else:
                    factor = jnp.exp2(old - new)
                    l_ref[row : row + 1, :] = l_ref[row : row + 1, :] * factor + total
                    acc[64 * row : 64 * row + 64, :] = acc[64 * row : 64 * row + 64, :] * factor + o
                m_ref[row : row + 1, :] = new

    attend(2 * b, 2 * b + 1, True)

    def first_plane(i, _):
        orgs = []
        for f in range(2):
            major, minor = coords[f]
            pp, xx = plane(i, major, x)
            org = origin(f, pp, minor, xx)
            orgs.append(org)
            arrived(f, org)

            @pl.when((i == 1) | (i == 2))
            def _():
                copy(f, org, origin(f, (major + 1) % 4, minor, x), i, 2).start()

            @pl.when((i == 1) | (i == 5))
            def _():
                copy(f, org, origin(f, (major + 3) % 4, minor, x), i, 3).start()

            copy(f, org, origin(f, major, (minor + 1) % 4, x), i, 0).start()
            copy(f, org, origin(f, major, (minor + 3) % 4, x), i, 1).start()
        attend(2 * orgs[0], 2 * orgs[1] + 1, False)
        return 0

    lax.fori_loop(1, 8, first_plane, 0)

    def near(n, _):
        i, back = n // 2, (n + 1) % 2
        orgs = []
        for f in range(2):
            major, minor = coords[f]
            pp, xx = plane(i, major, x)
            org = origin(f, pp, (minor + 1 + 2 * back) % 4, xx)
            orgs.append(org)
            arrived(f, org)

            @pl.when(i % 2 == 1 - back)
            def _():
                copy(f, org, origin(f, major, (minor + 3 + 2 * back) % 4, x), i, 5).start()

        attend(2 * orgs[0], 2 * orgs[1] + 1, False)
        return 0

    lax.fori_loop(0, 16, near, 0)

    def far(i, _):
        orgs = []
        for f in range(2):
            major, minor = coords[f]
            pp, xx = plane(i, major, x)
            org = origin(f, pp, (minor + 2) % 4, xx)
            orgs.append(org)
            arrived(f, org)
        attend(2 * orgs[0], 2 * orgs[1] + 1, False)
        return 0

    lax.fori_loop(0, 8, far, 0)

    for n in range(8):
        inv = 1.0 / l_ref[n : n + 1, :]
        out[:, 64 * n : 64 * n + 64] = (acc[64 * n : 64 * n + 64, :] * inv).T.astype(jnp.bfloat16)

    def sent(i, _):
        for f in range(2):
            for which in (0, 1, 5):
                copy(f, b, peers[0], i, which).wait_send()
        return 0

    lax.fori_loop(0, 8, sent, 0)
    for f in range(2):
        for i, which in ((0, 4), (0, 2), (0, 3), (1, 2), (1, 3), (2, 2), (5, 3)):
            copy(f, b, peers[0], i, which).wait_send()


def attention(tok, gain, wq, wk, wv, cos, sin, bias, diag):
    vmem = pl.BlockSpec(memory_space=pltpu.VMEM)
    return pl.pallas_call(
        attention_kernel,
        out_shape=jax.ShapeDtypeStruct((256, 512), jnp.bfloat16),
        in_specs=[vmem] * 9,
        out_specs=vmem,
        scratch_shapes=[
            pltpu.VMEM((256, 2048), jnp.bfloat16),
            pltpu.VMEM((64, 256, 128), jnp.bfloat16),
            pltpu.VMEM((2, 4, 128, 256), jnp.bfloat16),
            pltpu.VMEM((8, 256), jnp.float32),
            pltpu.VMEM((8, 256), jnp.float32),
            pltpu.VMEM((512, 256), jnp.float32),
            pltpu.SemaphoreType.DMA((2, 8, 6)),
            pltpu.SemaphoreType.DMA((64,)),
        ],
        compiler_params=pltpu.CompilerParams(
            collective_id=0, has_side_effects=True, vmem_limit_bytes=48 * 1024 * 1024
        ),
        name="attention",
    )(tok, gain, wq, wk, wv, cos, sin, bias, diag)


def local(tokens, order, gain_attn, gain_ffn, w_query, w_key, w_value, w_out, w_gate, w_up, w_down):
    tok_rows, model_width = tokens.shape
    half_rows = tok_rows // 2
    b = lax.axis_index("blk")
    own = lax.dynamic_slice_in_dim(order, 2 * b, 2)
    block_of = jnp.repeat(own, half_rows)
    pos = block_of * half_rows + jnp.arange(tok_rows, dtype=jnp.int32) % half_rows
    freq = ROPE_BASE ** (-(jnp.arange(HD // 2, dtype=jnp.float32) * 2.0 / HD))
    angle = freq[:, None] * pos.astype(jnp.float32)[None, :]
    bias = jnp.where(order[:, None] > block_of[None, :], BIG, 0.0).astype(jnp.float32)
    diag = jnp.where(pos[:, None] <= pos[None, :], 0.0, -BIG).astype(jnp.float32)
    heads = attention(
        tokens, gain_attn[None, :], w_query, w_key, w_value, jnp.cos(angle), jnp.sin(angle), bias, diag
    )
    tokens_wide = tokens.astype(jnp.float32)
    partial_value = jnp.dot(heads, w_out, preferred_element_type=jnp.float32)
    share = model_width // lax.axis_size("tp")
    col_start = lax.axis_index("tp") * share
    attention_sum = gathered_total(partial_value.astype(jnp.bfloat16), "tp").astype(jnp.float32)
    resid_full = tokens_wide + attention_sum
    normed_ffn = (
        resid_full
        * lax.rsqrt(jnp.mean(resid_full * resid_full, axis=-1, keepdims=True) + EPS)
        * gain_ffn
    ).astype(jnp.bfloat16)
    gate = jnp.dot(normed_ffn, w_gate, preferred_element_type=jnp.float32)
    up_proj = jnp.dot(normed_ffn, w_up, preferred_element_type=jnp.float32)
    residual = lax.dynamic_slice_in_dim(resid_full, col_start, share, 1)
    hidden = (jax.nn.silu(gate) * up_proj).astype(jnp.bfloat16)
    down = jnp.dot(hidden, w_down, preferred_element_type=jnp.float32)
    feed = sum_at_owner(down.astype(jnp.bfloat16), "tp", 1)
    return (residual + feed).astype(jnp.bfloat16)


def solution(mesh):
    placed = (
        P("blk", None),
        P(),
        P(),
        P(),
        P(None, "tp"),
        P(None, "tp"),
        P(None, "tp"),
        P("tp", None),
        P(None, "tp"),
        P(None, "tp"),
        P("tp", None),
    )
    return jax.shard_map(
        local, mesh=mesh, in_specs=placed, out_specs=P("blk", "tp"), check_vma=False
    )
```

time: 277 us -> 191 us (0.69)
  Pallas kernels: 0 us -> 76.7 us
  waiting for transfers between devices: 136 us -> 60.5 us
  matrix products: 59 us -> 20.5 us
  local copies, waits for them, and re-layouts: 32 us -> 8.95 us
  other arithmetic: 29.5 us -> 6.76 us
    pallas_call x0 -> x1, Pallas kernels: none -> 76.7 us  [attention(): pl.pallas_call(attention_kernel, out_shape=jax.ShapeDtypeStruct((256, 512...]
    all_gather x1 -> x0, waiting for transfers between devices: 75.9 us -> none  [local(): piece = lax.all_gather(packed, 'blk', axis=0, tiled=True)]
    dot_general x35 -> x0, matrix products: 38.5 us -> none  [the longest x16 20.3 us: attend(): jnp.einsum('kgqs,skd->kgqd', weights.astype(jnp.bfloat16), value_block, p...]
    reduce_sum x19 -> x0, other arithmetic: 19 us -> none  [the longest x16 16.1 us: attend(): denominator = denominator * factor + jnp.sum(weights, axis=-1)]
    slice x16 -> x0, local copies, waits for them, and re-layouts: 15.9 us -> none  [attend(): value_block = block[:, kv_local * HD:].reshape(-1, kv_local, HD)]
    while x80 -> x0, local copies, waits for them, and re-layouts: 12.5 us -> none
    unnamed x14 -> x18, local copies, waits for them, and re-layouts: 1.35 us -> 6.93 us
  transfers between devices with their start and end apart: 3 -> 2, of which waited for: 3 -> 2; matrix products, arithmetic and copies ran while one was open for 1% -> 0% of each run, Pallas kernels for 0% -> 0%
where the time goes in v1:
time: 191 us; the launch traced here: 190 us
  Pallas kernels  76.7 us (40%)
  waiting for transfers between devices  60.5 us (32%)
  matrix products  20.5 us (11%)
  between operations  13.5 us (7%)
  local copies, waits for them, and re-layouts  8.95 us (5%)
  other arithmetic  6.76 us (4%)
  starting transfers between devices  3.51 us (2%)
    pallas_call x1, Pallas kernels, attention(): pl.pallas_call(attention_kernel, out_shape=jax.ShapeDtypeStruct((256, 512...  76.7 us
    all_gather x1, waiting for transfers between devices, gathered_total(): return lax.all_gather(shard, axis).astype(jnp.float32).sum(0)  47.5 us
    all_to_all x1, waiting for transfers between devices, sum_at_owner(): parts = lax.all_to_all(in_blocks(shard, dim, peers), axis, 0, 0, tiled=True)  13 us
    dot_general x1, matrix products, local(): down = jnp.dot(hidden, w_down, preferred_element_type=jnp.float32)  11.7 us
    dot_general x1, matrix products, local(): gate = jnp.dot(normed_ffn, w_gate, preferred_element_type=jnp.float32)  7.07 us
    unnamed x18, local copies, waits for them, and re-layouts  6.93 us
  transfers between devices with their start and end apart: 2, of which 2 were waited for; matrix products, arithmetic and copies ran while one was open for 0% of the time, Pallas kernels for 0%

profile of v1, /device:TPU:1, one launch (start us, length us, event | category | flops | bytes accessed | tf_op | source)
XLA Modules:
  0.0 190.4 jit_solution(4945113333196860004)
XLA Ops:
  6.6 0.9 dynamic_slice.6
  7.4 0.1 broadcast_bitcast_fusion
  7.5 0.1 fusion.4
  7.6 0.7 compare_select_fusion.1.bias
  8.3 0.1 compare_select_fusion.diag
  8.4 0.2 multiply_sine_fusion
  8.6 1.2 copy-done.1
  9.8 1.6 copy-done.3
  11.4 1.0 copy-done.4
  12.5 1.0 copy-done.5
  13.5 0.7 copy-done.6
  14.2 76.7 %attention.1 = bf16[256,512]{1,0:T(8,128)(2,1)S(1)} custom-call(bf16[256,2048]{1,0:T(8,128)(2,1)S(1)} %copy-done.1, f32[1,2048]{1,0:T(1,128)S(1)} %bitcast.19, bf16[2048,512]{1,0:T(8,128)(2,1)S(1)} %copy-done.3, bf16[2048,128]{1,0:T(8,128)(2,1)S(1)} %copy-done.4, bf16[2048,128]{1,0:T(8,128)(2,1)S(1)} %copy-done.5, f32[32,256]{1,0:T(8,128)S(1)} %get-tuple-element.10.cos, ...), custom_call_target="tpu_custom_call" | custom-call | tf_op jit(solution)/shard_map/attention/pallas_call | solution.py:244
  90.9 1.7 convolution_convert_fusion
  92.6 47.5 %all-gather.3.cloned.1.call-done = bf16[1024,2048]{1,0:T(8,128)(2,1)} async-done(((bf16[256,2048]{1,0:T(8,128)(2,1)}), bf16[1024,2048]{1,0:T(8,128)(2,1)}) %all-gather.3.cloned.1.call-update) | async-done | bytes 4194320 | tf_op jit(solution)/shard_map/all_gather | solution.py:19
  140.2 3.3 %convert_reduce_fusion = f32[256,2048]{1,0:T(8,128)S(1)} fusion(bf16[4,256,2048]{2,1,0:T(8,128)(2,1)} %bitcast.20), kind=kLoop, calls=%fused_computation | loop fusion | flops 3670016 | bytes 6291456 | tf_op jit(solution)/shard_map/reduce_sum | solution.py:19
  143.5 0.4 multiply_reduce_fusion
  143.9 1.3 copy-done.7
  145.2 7.1 %fusion.3 = f32[256,2048]{1,0:T(8,128)} fusion(bf16[2048,2048]{1,0:T(8,128)(2,1)} %param.19, f32[256,2048]{1,0:T(8,128)S(1)} %get-tuple-element.6, f32[2048]{0:T(1024)S(1)} %copy-done.8, f32[256]{0:T(256)S(1)} %add_rsqrt_fusion), kind=kOutput, calls=%fused_computation.21 | convolution fusion | flops 2149056512 | bytes 12592128 | tf_op jit(solution)/shard_map/dot_general | solution.py:291
  152.3 11.7 %convolution_convert_fusion.1 = bf16[256,2048]{1,0:T(8,128)(2,1)S(1)} fusion(bf16[2048,2048]{1,0:T(8,128)(2,1)} %param.21, bf16[2048,2048]{1,0:T(8,128)(2,1)} %param.20, f32[256,2048]{1,0:T(8,128)} %fusion.3, f32[256,2048]{1,0:T(8,128)} %copy-done.7, f32[2048]{0:T(1024)S(1)} %copy-done.8, f32[256]{0:T(256)S(1)} %add_rsqrt_fusion), kind=kOutput, calls=%fused_computation.4 | convolution fusion | flops 4300210176 | bytes 22029312 | tf_op jit(solution)/shard_map/dot_general | solution.py:295
  164.0 1.1 copy.15
  165.1 3.5 %all-to-all-start = ((bf16[4,256,512]{2,1,0:T(8,128)(2,1)}), bf16[4,256,512]{2,1,0:T(8,128)(2,1)S(1)}, u32[]{:S(2)}, u32[]{:S(2)}) async-start(bf16[4,256,512]{2,1,0:T(8,128)(2,1)} %bitcast.21), calls=%async_computation | async-start | bytes 2097152 | tf_op jit(solution)/shard_map/all_to_all | solution.py:29
  168.6 13.0 %all-to-all-done = bf16[4,256,512]{2,1,0:T(8,128)(2,1)S(1)} async-done(((bf16[4,256,512]{2,1,0:T(8,128)(2,1)}), bf16[4,256,512]{2,1,0:T(8,128)(2,1)S(1)}, u32[]{:S(2)}, u32[]{:S(2)}) %all-to-all-start) | async-done | bytes 1048608 | tf_op jit(solution)/shard_map/all_to_all | solution.py:29
  181.6 0.1 convert_reduce_fusion.1
  181.7 1.8 add_convert_fusion
  (16 shorter events, 0.1 us)
Async XLA Ops:
  6.5 84.4 %copy-start = (bf16[512,2048]{1,0:T(8,128)(2,1)S(1)}, bf16[512,2048]{1,0:T(8,128)(2,1)}, u32[]{:S(2)}) copy-start(bf16[512,2048]{1,0:T(8,128)(2,1)} %param.18) | copy-start | bytes 6291460
  6.5 133.6 %all-gather.3.cloned.1.call-start = ((), (), s32[]{:S(2)}) async-start(), calls=%async_computation.1 | async-start | bytes 5242880 | tf_op jit(solution)/shard_map/all_gather | solution.py:19
  8.6 1.2 copy-start.1
  9.8 1.6 copy-start.3
  11.4 1.0 copy-start.4
  12.5 1.0 copy-start.5
  13.5 0.7 copy-start.6
  140.2 3.3 %copy-start.2 = (bf16[256,2048]{1,0:T(8,128)(2,1)S(1)}, bf16[256,2048]{1,0:T(8,128)(2,1)}, u32[]{:S(2)}) copy-start(bf16[256,2048]{1,0:T(8,128)(2,1)} %tok.1) | copy-start | bytes 3145732
  143.5 1.7 copy-start.8
  143.9 1.3 copy-start.7
  165.1 16.5 %all-to-all-start = ((bf16[4,256,512]{2,1,0:T(8,128)(2,1)}), bf16[4,256,512]{2,1,0:T(8,128)(2,1)S(1)}, u32[]{:S(2)}, u32[]{:S(2)}) async-start(bf16[4,256,512]{2,1,0:T(8,128)(2,1)} %bitcast.21), calls=%async_computation | async-start | bytes 2097152 | tf_op jit(solution)/shard_map/all_to_all | solution.py:29
Sparse Core Ops, SparseCore 0:
  92.8 47.3 all-gather.2

commit v2 on v1

v2 whole, which is shorter than its diff:
```python
import jax
import jax.numpy as jnp
from jax import lax
from jax.experimental import pallas as pl
from jax.experimental.pallas import tpu as pltpu
from jax.sharding import PartitionSpec as P

HD = 64
SHARE = 512
CHUNKS = 2
ROWS = 256 // CHUNKS
EPS = 1e-05
ROPE_BASE = 500000.0
BIG = 1e30
LOG2E = 1.4426950408889634
MESH = pl.DeviceIdType.MESH


def origin(flow, major, minor, x):
    if flow == 0:
        return minor * 8 + major * 2 + x
    return major * 8 + minor * 2 + x


def plane(i, major, x):
    k = i // 2
    step = (3 * k + 3 * (k // 2) + 2 * (k // 3)) % 4
    return (major + step) % 4, (x + i) % 2


def layer_kernel(
    tok_hbm, gain, wq_hbm, wk_hbm, wv_hbm, cos, sin, bias, diag, gain2, wo_hbm, wg_hbm, wu_hbm, wd_hbm,
    out, tok, wq, wk, wv, wo, wg, wu, wd, heads, near_out, near_in, far_out, far_in, kept, resid,
    shares, hidden, load_sem, tail_send, tail_recv, normed, kv, qp, s_ref, mo_ref, f_ref, m_ref, l_ref, acc, send_sem, recv_sem,
):
    b = lax.axis_index("blk")
    z, y, x = b // 8, (b // 2) % 4, b % 2
    coords = ((y, z), (z, y))

    t = lax.axis_index("tp")
    core = t % 2
    twin = t + 1 - 2 * core
    across = (t + 2) % 4
    loads = [
        pltpu.make_async_copy(src, dst, load_sem.at[i])
        for i, (src, dst) in enumerate(
            ((tok_hbm, tok), (wk_hbm, wk), (wv_hbm, wv), (wq_hbm, wq))
            + ((wo_hbm, wo), (wg_hbm, wg), (wu_hbm, wu), (wd_hbm, wd))
        )
    ]
    for load in loads[:4]:
        load.start()
    barrier = pltpu.get_barrier_semaphore()
    for peer in (twin, across):
        pl.semaphore_signal(barrier, inc=1, device_id={"tp": peer}, device_id_type=MESH)
    peers = [origin(0, y, z, (x + 1) % 2)]
    peers += [origin(0, (y + d) % 4, z, x) for d in (1, 3)]
    peers += [origin(0, y, (z + d) % 4, x) for d in (1, 3)]
    for peer in peers:
        pl.semaphore_signal(barrier, inc=1, device_id={"blk": peer}, device_id_type=MESH)

    rows = 64
    loads[0].wait()

    def norm_rows(r, _):
        at = pl.ds(pl.multiple_of(r * rows, rows), rows)
        t = tok[at, :].astype(jnp.float32)
        scale = lax.rsqrt(jnp.mean(t * t, axis=-1, keepdims=True) + EPS)
        normed[at, :] = (t * scale * gain[...]).astype(jnp.bfloat16)
        return 0

    lax.fori_loop(0, 256 // rows, norm_rows, 0)

    c = cos[...]
    s = sin[...]

    def rotated(u):
        a, h = u[0:32], u[32:64]
        return jnp.concatenate([a * c - h * s, h * c + a * s], axis=0)

    loads[1].wait()
    loads[2].wait()
    k = jnp.dot(normed[...], wk[...], preferred_element_type=jnp.float32).T
    kt = jnp.concatenate([rotated(k[0:64]), rotated(k[64:128])], axis=0)
    kn = kt.T.astype(jnp.bfloat16)
    v = jnp.dot(normed[...], wv[...], preferred_element_type=jnp.float32).T.astype(jnp.bfloat16)
    for f in range(2):
        kv[2 * b + f, 0:128, :] = kn[128 * f : 128 * f + 128, :]
        kv[2 * b + f, 128:256, :] = v[:, 128 * f : 128 * f + 128]

    pl.semaphore_wait(barrier, 7)

    def copy(f, org, dest, i, which):
        unit = 2 * org + f
        return pltpu.make_async_remote_copy(
            src_ref=kv.at[unit], dst_ref=kv.at[unit],
            send_sem=send_sem.at[f, i, which], recv_sem=recv_sem.at[unit],
            device_id={"blk": dest}, device_id_type=MESH,
        )

    def arrived(f, org):
        unit = 2 * org + f
        pltpu.make_async_remote_copy(
            src_ref=kv.at[unit], dst_ref=kv.at[unit],
            send_sem=send_sem.at[f, 0, 0], recv_sem=recv_sem.at[unit],
            device_id={"blk": peers[0]}, device_id_type=MESH,
        ).wait_recv()

    for f in range(2):
        major, minor = coords[f]
        copy(f, b, origin(f, major, minor, (x + 1) % 2), 0, 4).start()
    for f in range(2):
        major, minor = coords[f]
        copy(f, b, origin(f, (major + 1) % 4, minor, x), 0, 2).start()
        copy(f, b, origin(f, (major + 3) % 4, minor, x), 0, 3).start()
    for f in range(2):
        major, minor = coords[f]
        copy(f, b, origin(f, major, (minor + 1) % 4, x), 0, 0).start()
        copy(f, b, origin(f, major, (minor + 3) % 4, x), 0, 1).start()

    loads[3].wait()
    for load in loads[4:]:
        load.start()
    zero = jnp.zeros((64, 256), jnp.bfloat16)
    for half in range(2):
        q = jnp.dot(
            normed[...], wq[:, 256 * half : 256 * half + 256], preferred_element_type=jnp.float32
        ).T
        for n in range(4):
            u = (rotated(q[64 * n : 64 * n + 64]) * (HD**-0.5 * LOG2E)).astype(jnp.bfloat16)
            top, low = (u, zero) if half == 0 else (zero, u)
            qp[half, n, 0:64, :] = top
            qp[half, n, 64:128, :] = low

    def weigh(row, ja, jb, first):
        g, n = row // 4, row % 4
        pa = jnp.exp2(s_ref[row, 0:128, :] - mo_ref[0, row : row + 1, :])
        pb = jnp.exp2(s_ref[row, 128:256, :] - mo_ref[1, row : row + 1, :])
        total = jnp.sum(pa, axis=0, keepdims=True) + jnp.sum(pb, axis=0, keepdims=True)
        p = jnp.concatenate([pa, pb], axis=0).astype(jnp.bfloat16)
        va = kv[ja, 128 + 64 * g : 192 + 64 * g, :]
        vb = kv[jb, 128 + 64 * g : 192 + 64 * g, :]
        o = jnp.dot(jnp.concatenate([va, vb], axis=1), p, preferred_element_type=jnp.float32)
        if first:
            l_ref[row : row + 1, :] = total
            acc[64 * row : 64 * row + 64, :] = o
        else:
            factor = f_ref[row : row + 1, :]
            l_ref[row : row + 1, :] = l_ref[row : row + 1, :] * factor + total
            acc[64 * row : 64 * row + 64, :] = acc[64 * row : 64 * row + 64, :] * factor + o

    def score(row, ja, jb, first):
        g, n = row // 4, row % 4
        sa = jnp.dot(kv[ja, 0:128, :], qp[g, n], preferred_element_type=jnp.float32)
        sb = jnp.dot(kv[jb, 0:128, :], qp[g, n], preferred_element_type=jnp.float32)
        if first:
            sa = sa + diag[0:128, :]
            sb = sb + diag[128:256, :]
        s_ref[row, 0:128, :] = sa
        s_ref[row, 128:256, :] = sb
        ma, mb = jnp.max(sa, axis=0, keepdims=True), jnp.max(sb, axis=0, keepdims=True)
        if first:
            new = jnp.maximum(ma, mb)
            mo_ref[0, row : row + 1, :] = new
            mo_ref[1, row : row + 1, :] = new
        else:
            ba, bb = bias[pl.ds(ja, 1), :], bias[pl.ds(jb, 1), :]
            old = m_ref[row : row + 1, :]
            new = jnp.maximum(old, jnp.maximum(ma - ba, mb - bb))
            f_ref[row : row + 1, :] = jnp.exp2(old - new)
            mo_ref[0, row : row + 1, :] = new + ba
            mo_ref[1, row : row + 1, :] = new + bb
        m_ref[row : row + 1, :] = new

    def attend(before, now):
        for row in range(8):
            weigh(row, *before, False)
            score(row, *now, False)
        return now

    for row in range(8):
        score(row, 2 * b, 2 * b + 1, True)
    for row in range(8):
        l_ref[row : row + 1, :] = jnp.zeros((1, 256), jnp.float32)
        acc[64 * row : 64 * row + 64, :] = jnp.zeros((64, 256), jnp.float32)
        f_ref[row : row + 1, :] = jnp.zeros((1, 256), jnp.float32)
    held = (2 * b, 2 * b + 1)

    def first_plane(i, held):
        orgs = []
        for f in range(2):
            major, minor = coords[f]
            pp, xx = plane(i, major, x)
            org = origin(f, pp, minor, xx)
            orgs.append(org)
            arrived(f, org)

            @pl.when((i == 1) | (i == 2))
            def _():
                copy(f, org, origin(f, (major + 1) % 4, minor, x), i, 2).start()

            @pl.when((i == 1) | (i == 5))
            def _():
                copy(f, org, origin(f, (major + 3) % 4, minor, x), i, 3).start()

            copy(f, org, origin(f, major, (minor + 1) % 4, x), i, 0).start()
            copy(f, org, origin(f, major, (minor + 3) % 4, x), i, 1).start()
        return attend(held, (2 * orgs[0], 2 * orgs[1] + 1))

    held = lax.fori_loop(1, 8, first_plane, held)

    def near(n, held):
        i, back = n // 2, (n + 1) % 2
        orgs = []
        for f in range(2):
            major, minor = coords[f]
            pp, xx = plane(i, major, x)
            org = origin(f, pp, (minor + 1 + 2 * back) % 4, xx)
            orgs.append(org)
            arrived(f, org)

            @pl.when(i % 2 == 1 - back)
            def _():
                copy(f, org, origin(f, major, (minor + 3 + 2 * back) % 4, x), i, 5).start()

        return attend(held, (2 * orgs[0], 2 * orgs[1] + 1))

    held = lax.fori_loop(0, 16, near, held)

    def far(i, held):
        orgs = []
        for f in range(2):
            major, minor = coords[f]
            pp, xx = plane(i, major, x)
            org = origin(f, pp, (minor + 2) % 4, xx)
            orgs.append(org)
            arrived(f, org)
        return attend(held, (2 * orgs[0], 2 * orgs[1] + 1))

    held = lax.fori_loop(0, 8, far, held)
    for row in range(8):
        weigh(row, *held, False)

    for n in range(8):
        inv = 1.0 / l_ref[n : n + 1, :]
        heads[:, 64 * n : 64 * n + 64] = (acc[64 * n : 64 * n + 64, :] * inv).T.astype(jnp.bfloat16)

    def sent(i, _):
        for f in range(2):
            for which in (0, 1, 5):
                copy(f, b, peers[0], i, which).wait_send()
        return 0

    lax.fori_loop(0, 8, sent, 0)
    for f in range(2):
        for i, which in ((0, 4), (0, 2), (0, 3), (1, 2), (1, 3), (2, 2), (5, 3)):
            copy(f, b, peers[0], i, which).wait_send()

    def tail_copy(stage, r, src, dst, peer):
        return pltpu.make_async_remote_copy(
            src_ref=src, dst_ref=dst,
            send_sem=tail_send.at[stage, r], recv_sem=tail_recv.at[stage, r],
            device_id={"tp": peer}, device_id_type=MESH,
        )

    def columns(c):
        return pl.ds(pl.multiple_of(c * SHARE, SHARE), SHARE)

    def project(stage, r, lhs, w):
        for j, c in enumerate((1 - core, 3 - core)):
            part = jnp.dot(lhs, w[:, columns(c)], preferred_element_type=jnp.float32)
            near_out[stage, r, j] = part.astype(jnp.bfloat16)
        tail_copy(2 * stage, r, near_out.at[stage, r], near_in.at[stage, r], twin).start()
        for j, c in enumerate((across, t)):
            kept[r, j] = jnp.dot(lhs, w[:, columns(c)], preferred_element_type=jnp.float32)

    def cross(stage, r):
        tail_copy(2 * stage, r, near_out.at[stage, r], near_in.at[stage, r], twin).wait()
        far = 1 - t // 2
        far_out[stage, r] = (kept[r, 0] + near_in[stage, r, far].astype(jnp.float32)).astype(jnp.bfloat16)
        tail_copy(2 * stage + 1, r, far_out.at[stage, r], far_in.at[stage, r], across).start()
        kept[r, 1] = kept[r, 1] + near_in[stage, r, 1 - far].astype(jnp.float32)

    def total(stage, r):
        tail_copy(2 * stage + 1, r, far_out.at[stage, r], far_in.at[stage, r], across).wait()
        return kept[r, 1] + far_in[stage, r].astype(jnp.float32)

    def share_copy(stage, r, slot, peer):
        return tail_copy(stage, r, shares.at[r, slot], shares.at[r, slot], peer)

    loads[4].wait()
    for r in range(CHUNKS):
        project(0, r, heads[ROWS * r : ROWS * r + ROWS, :], wo)
    for r in range(CHUNKS):
        cross(0, r)
    for r in range(CHUNKS):
        at = slice(ROWS * r, ROWS * r + ROWS)
        own = tok[at, columns(t)].astype(jnp.float32) + total(0, r)
        resid[at, :] = own
        shares[r, t] = own.astype(jnp.bfloat16)
        share_copy(4, r, t, across).start()
        share_copy(5, r, t, twin).start()
    for load in loads[5:]:
        load.wait()

    def feed_forward(r):
        share_copy(4, r, across, across).wait_recv()
        share_copy(6, r, across, twin).start()
        share_copy(5, r, twin, twin).wait_recv()
        share_copy(6, r, (twin + 2) % 4, twin).wait_recv()
        squares = jnp.zeros((ROWS, 1), jnp.float32)
        for c in range(4):
            u = shares[r, c].astype(jnp.float32)
            squares = squares + jnp.sum(u * u, axis=-1, keepdims=True)
        scale = lax.rsqrt(squares * (1.0 / (4 * SHARE)) + EPS)
        for c in range(4):
            u = shares[r, c].astype(jnp.float32)
            at = slice(SHARE * c, SHARE * c + SHARE)
            normed[ROWS * r : ROWS * r + ROWS, at] = (u * scale * gain2[:, at]).astype(jnp.bfloat16)

        def units(n, _):
            at = pl.ds(pl.multiple_of(n * 256, 256), 256)
            u = normed[ROWS * r : ROWS * r + ROWS, :]
            gate = jnp.dot(u, wg[:, at], preferred_element_type=jnp.float32)
            up = jnp.dot(u, wu[:, at], preferred_element_type=jnp.float32)
            hidden[r, :, at] = (gate / (1.0 + jnp.exp(-gate)) * up).astype(jnp.bfloat16)
            return 0

        lax.fori_loop(0, 8, units, 0)
        project(1, r, hidden[r], wd)

    for r in range(CHUNKS):
        feed_forward(r)
        if r > 0:
            cross(1, r - 1)
    cross(1, CHUNKS - 1)
    for r in range(CHUNKS):
        at = slice(ROWS * r, ROWS * r + ROWS)
        out[at, :] = (resid[at, :] + total(1, r)).astype(jnp.bfloat16)
    for r in range(CHUNKS):
        share_copy(4, r, t, across).wait_send()
        share_copy(5, r, t, twin).wait_send()
        share_copy(6, r, across, twin).wait_send()


def layer(tok, gain, wq, wk, wv, cos, sin, bias, diag, gain2, wo, wg, wu, wd):
    vmem = pl.BlockSpec(memory_space=pltpu.VMEM)
    hbm = pl.BlockSpec(memory_space=pl.ANY)
    bf16, f32 = jnp.bfloat16, jnp.float32
    return pl.pallas_call(
        layer_kernel,
        out_shape=jax.ShapeDtypeStruct((256, SHARE), bf16),
        in_specs=[hbm, vmem, hbm, hbm, hbm, vmem, vmem, vmem, vmem, vmem, hbm, hbm, hbm, hbm],
        out_specs=vmem,
        scratch_shapes=[
            pltpu.VMEM((256, 2048), bf16),
            pltpu.VMEM((2048, 512), bf16),
            pltpu.VMEM((2048, 128), bf16),
            pltpu.VMEM((2048, 128), bf16),
            pltpu.VMEM((512, 2048), bf16),
            pltpu.VMEM((2048, 2048), bf16),
            pltpu.VMEM((2048, 2048), bf16),
            pltpu.VMEM((2048, 2048), bf16),
            pltpu.VMEM((256, 512), bf16),
            pltpu.VMEM((2, CHUNKS, 2, ROWS, SHARE), bf16),
            pltpu.VMEM((2, CHUNKS, 2, ROWS, SHARE), bf16),
            pltpu.VMEM((2, CHUNKS, ROWS, SHARE), bf16),
            pltpu.VMEM((2, CHUNKS, ROWS, SHARE), bf16),
            pltpu.VMEM((CHUNKS, 2, ROWS, SHARE), f32),
            pltpu.VMEM((256, SHARE), f32),
            pltpu.VMEM((CHUNKS, 4, ROWS, SHARE), bf16),
            pltpu.VMEM((CHUNKS, ROWS, 2048), bf16),
            pltpu.SemaphoreType.DMA((8,)),
            pltpu.SemaphoreType.DMA((7, CHUNKS)),
            pltpu.SemaphoreType.DMA((7, CHUNKS)),
            pltpu.VMEM((256, 2048), bf16),
            pltpu.VMEM((64, 256, 128), bf16),
            pltpu.VMEM((2, 4, 128, 256), bf16),
            pltpu.VMEM((8, 256, 256), f32),
            pltpu.VMEM((2, 8, 256), f32),
            pltpu.VMEM((8, 256), f32),
            pltpu.VMEM((8, 256), f32),
            pltpu.VMEM((8, 256), f32),
            pltpu.VMEM((512, 256), f32),
            pltpu.SemaphoreType.DMA((2, 8, 6)),
            pltpu.SemaphoreType.DMA((64,)),
        ],
        compiler_params=pltpu.CompilerParams(
            collective_id=0, has_side_effects=True, vmem_limit_bytes=62 * 1024 * 1024
        ),
        name="layer",
    )(tok, gain, wq, wk, wv, cos, sin, bias, diag, gain2, wo, wg, wu, wd)


def local(tokens, order, gain_attn, gain_ffn, w_query, w_key, w_value, w_out, w_gate, w_up, w_down):
    tok_rows = tokens.shape[0]
    half_rows = tok_rows // 2
    b = lax.axis_index("blk")
    own = lax.dynamic_slice_in_dim(order, 2 * b, 2)
    block_of = jnp.repeat(own, half_rows)
    pos = block_of * half_rows + jnp.arange(tok_rows, dtype=jnp.int32) % half_rows
    freq = ROPE_BASE ** (-(jnp.arange(HD // 2, dtype=jnp.float32) * 2.0 / HD))
    angle = freq[:, None] * pos.astype(jnp.float32)[None, :]
    bias = jnp.where(order[:, None] > block_of[None, :], BIG, 0.0).astype(jnp.float32)
    diag = jnp.where(pos[:, None] <= pos[None, :], 0.0, -BIG).astype(jnp.float32)
    return layer(
        tokens, gain_attn[None, :], w_query, w_key, w_value, jnp.cos(angle), jnp.sin(angle), bias, diag,
        gain_ffn[None, :], w_out, w_gate, w_up, w_down,
    )


def solution(mesh):
    placed = (
        P("blk", None),
        P(),
        P(),
        P(),
        P(None, "tp"),
        P(None, "tp"),
        P(None, "tp"),
        P("tp", None),
        P(None, "tp"),
        P(None, "tp"),
        P("tp", None),
    )
    return jax.shard_map(
        local, mesh=mesh, in_specs=placed, out_specs=P("blk", "tp"), check_vma=False
    )
```

time: 191 us -> 82.8 us (0.43)
  waiting for transfers between devices: 60.5 us -> 0 us
  matrix products: 20.5 us -> 0 us
  between operations: 13.5 us -> 0.01 us
  local copies, waits for them, and re-layouts: 8.95 us -> 2.47 us
  other arithmetic: 6.76 us -> 3.08 us
  starting transfers between devices: 3.51 us -> 0 us
    all_gather x1 -> x0, waiting for transfers between devices: 47.5 us -> none  [gathered_total(): return lax.all_gather(shard, axis).astype(jnp.float32).sum(0)]
    dot_general x3 -> x0, matrix products: 20.5 us -> none  [the longest x1 11.7 us: local(): down = jnp.dot(hidden, w_down, preferred_element_type=jnp.float32)]
    all_to_all x1 -> x0, waiting for transfers between devices: 13 us -> none  [sum_at_owner(): parts = lax.all_to_all(in_blocks(shard, dim, peers), axis, 0, 0, tiled=True)]
    unnamed x18 -> x1, local copies, waits for them, and re-layouts: 6.93 us -> 1.67 us
    reduce_sum x3 -> x0, other arithmetic: 3.83 us -> none  [the longest x1 3.32 us: gathered_total(): return lax.all_gather(shard, axis).astype(jnp.float32).sum(0)]
    all_to_all x1 -> x0, starting transfers between devices: 3.5 us -> none  [sum_at_owner(): parts = lax.all_to_all(in_blocks(shard, dim, peers), axis, 0, 0, tiled=True)]
  transfers between devices with their start and end apart: 2 -> 0, of which waited for: 2 -> 0; matrix products, arithmetic and copies ran while one was open for 0% -> 0% of each run, Pallas kernels for 0% -> 0%
where the time goes in v2:
time: 82.8 us; the launch traced here: 82.5 us
  Pallas kernels  76.9 us (93%)
  other arithmetic  3.08 us (4%)
  local copies, waits for them, and re-layouts  2.47 us (3%)
    pallas_call x1, Pallas kernels, layer(): pl.pallas_call(layer_kernel, out_shape=jax.ShapeDtypeStruct((256, SHARE),...  76.9 us
    unnamed x1, local copies, waits for them, and re-layouts  1.67 us

profile of v2, /device:TPU:1, one launch (start us, length us, event | category | flops | bytes accessed | tf_op | source)
XLA Modules:
  0.0 82.5 jit_solution(4339732622410597434)
XLA Ops:
  0.0 0.7 dynamic_slice.3
  0.7 0.1 broadcast_bitcast_fusion
  0.8 0.1 fusion.1
  0.9 0.8 %multiply_sine_fusion = (f32[32,256]{1,0:T(8,128)}, f32[32,256]{1,0:T(8,128)}) fusion(f32[256]{0:T(256)S(1)} %get-tuple-element.5, f32[32]{0:T(128)S(1)} %negate_power_fusion), kind=kLoop, calls=%fused_computation.2 | loop fusion | flops 8192 | bytes 66688 | tf_op jit(solution)/shard_map/sin | solution.py:407
  1.7 1.4 %compare_select_fusion.1.bias = f32[64,256]{1,0:T(8,128)} fusion(s32[256]{0:T(256)S(1)} %broadcast_bitcast_fusion, s32[64]{0:T(128)} %param.12), kind=kLoop, calls=%fused_computation.1 | loop fusion | flops 32768 | bytes 66816 | tf_op jit(solution)/shard_map/jit(_where)/select_n | solution.py:404
  3.1 0.8 compare_select_fusion.diag
  3.9 76.9 %layer.1 = bf16[256,512]{1,0:T(8,128)(2,1)} custom-call(bf16[256,2048]{1,0:T(8,128)(2,1)} %tok_hbm.1, f32[1,2048]{1,0:T(1,128)} %bitcast.6, bf16[2048,512]{1,0:T(8,128)(2,1)} %wq_hbm.1, bf16[2048,128]{1,0:T(8,128)(2,1)} %wk_hbm.1, bf16[2048,128]{1,0:T(8,128)(2,1)} %wv_hbm.1, f32[32,256]{1,0:T(8,128)} %get-tuple-element.8.cos, ...), custom_call_target="tpu_custom_call" | custom-call | tf_op jit(solution)/shard_map/layer/pallas_call | solution.py:350
  80.8 1.7 %copy.13 = bf16[256,512]{1,0:T(8,128)(2,1)} copy(bf16[256,512]{1,0:T(8,128)(2,1)} %layer.1) | data formatting | bytes 524288
  (1 shorter events, 0.0 us)

commit v3 on v2

v3 whole, which is shorter than its diff:
```python
import jax
import jax.numpy as jnp
import numpy as np
from jax import lax
from jax.experimental import pallas as pl
from jax.experimental.pallas import tpu as pltpu
from jax.sharding import PartitionSpec as P

HD = 64
SHARE = 512
CHUNKS = 2
ROWS = 256 // CHUNKS
PIECE = 64
UNITS = 512
EPS = 1e-05
ROPE_BASE = 500000.0
BIG = 1e30
LOG2E = 1.4426950408889634
MESH = pl.DeviceIdType.MESH


def rope_table():
    freq = ROPE_BASE ** (-np.arange(HD // 2) * 2.0 / HD)[:, None]
    within = freq * np.arange(128)[None, :]
    starts = freq * (128.0 * np.arange(128))[None, :]
    return np.concatenate([np.cos(within), np.sin(within), np.cos(starts), np.sin(starts)]).astype(np.float32)


def origin(flow, major, minor, x):
    if flow == 0:
        return minor * 8 + major * 2 + x
    return major * 8 + minor * 2 + x


def plane(i, major, x):
    k = i // 2
    step = (3 * k + 3 * (k // 2) + 2 * (k // 3)) % 4
    return (major + step) % 4, (x + i) % 2


def layer_kernel(
    tok_hbm, order, gain, wq_hbm, wk_hbm, wv_hbm, tab, gain2, wo_hbm, wg_hbm, wu_hbm, wd_hbm,
    out, diag, blocks, gated, squares, tok, wq, wk, wv, wo, wg, wu, wd, heads, near_out, near_in, far_out, far_in, kept, resid,
    shares, hidden, load_sem, tail_send, tail_recv, normed, kv, qp, s_ref, mo_ref, f_ref, m_ref, l_ref, acc, send_sem, recv_sem,
):
    b = lax.axis_index("blk")
    z, y, x = b // 8, (b // 2) % 4, b % 2
    coords = ((y, z), (z, y))

    t = lax.axis_index("tp")
    core = t % 2
    twin = t + 1 - 2 * core
    across = (t + 2) % 4
    loads = [
        pltpu.make_async_copy(src, dst, load_sem.at[i])
        for i, (src, dst) in enumerate(
            ((tok_hbm, tok), (wk_hbm, wk), (wv_hbm, wv), (wq_hbm, wq))
            + ((wo_hbm, wo), (wg_hbm, wg), (wu_hbm, wu), (wd_hbm, wd))
        )
    ]
    for load in loads[:4]:
        load.start()
    barrier = pltpu.get_barrier_semaphore()
    for peer in (twin, across):
        pl.semaphore_signal(barrier, inc=1, device_id={"tp": peer}, device_id_type=MESH)
    peers = [origin(0, y, z, (x + 1) % 2)]
    peers += [origin(0, (y + d) % 4, z, x) for d in (1, 3)]
    peers += [origin(0, y, (z + d) % 4, x) for d in (1, 3)]
    for peer in peers:
        pl.semaphore_signal(barrier, inc=1, device_id={"blk": peer}, device_id_type=MESH)

    rows = 64
    loads[0].wait()

    def norm_rows(r, _):
        at = pl.ds(pl.multiple_of(r * rows, rows), rows)
        t = tok[at, :].astype(jnp.float32)
        scale = lax.rsqrt(jnp.mean(t * t, axis=-1, keepdims=True) + EPS)
        normed[at, :] = (t * scale * gain[...]).astype(jnp.bfloat16)
        return 0

    lax.fori_loop(0, 256 // rows, norm_rows, 0)

    first, second = order[2 * b], order[2 * b + 1]
    lane = lax.broadcasted_iota(jnp.int32, (32, 128), 1)
    cosines, sines = [], []
    for block in (first, second):
        ca = jnp.sum(jnp.where(lane == block, tab[64:96, :], 0.0), axis=1, keepdims=True)
        sa = jnp.sum(jnp.where(lane == block, tab[96:128, :], 0.0), axis=1, keepdims=True)
        cosines.append(ca * tab[0:32, :] - sa * tab[32:64, :])
        sines.append(sa * tab[0:32, :] + ca * tab[32:64, :])
    c = jnp.concatenate(cosines, axis=1)
    s = jnp.concatenate(sines, axis=1)

    def rotated(u):
        a, h = u[0:32], u[32:64]
        return jnp.concatenate([a * c - h * s, h * c + a * s], axis=0)

    loads[1].wait()
    loads[2].wait()
    k = jnp.dot(normed[...], wk[...], preferred_element_type=jnp.float32).T
    kt = jnp.concatenate([rotated(k[0:64]), rotated(k[64:128])], axis=0)
    kn = kt.T.astype(jnp.bfloat16)
    v = jnp.dot(normed[...], wv[...], preferred_element_type=jnp.float32).T.astype(jnp.bfloat16)
    for f in range(2):
        kv[2 * b + f, 0:128, :] = kn[128 * f : 128 * f + 128, :]
        kv[2 * b + f, 128:256, :] = v[:, 128 * f : 128 * f + 128]

    pl.semaphore_wait(barrier, 7)

    def copy(f, org, dest, i, which):
        unit = 2 * org + f
        return pltpu.make_async_remote_copy(
            src_ref=kv.at[unit], dst_ref=kv.at[unit],
            send_sem=send_sem.at[f, i, which], recv_sem=recv_sem.at[unit],
            device_id={"blk": dest}, device_id_type=MESH,
        )

    def arrived(f, org):
        unit = 2 * org + f
        pltpu.make_async_remote_copy(
            src_ref=kv.at[unit], dst_ref=kv.at[unit],
            send_sem=send_sem.at[f, 0, 0], recv_sem=recv_sem.at[unit],
            device_id={"blk": peers[0]}, device_id_type=MESH,
        ).wait_recv()

    for f in range(2):
        major, minor = coords[f]
        copy(f, b, origin(f, major, minor, (x + 1) % 2), 0, 4).start()
    for f in range(2):
        major, minor = coords[f]
        copy(f, b, origin(f, (major + 1) % 4, minor, x), 0, 2).start()
        copy(f, b, origin(f, (major + 3) % 4, minor, x), 0, 3).start()
    for f in range(2):
        major, minor = coords[f]
        copy(f, b, origin(f, major, (minor + 1) % 4, x), 0, 0).start()
        copy(f, b, origin(f, major, (minor + 3) % 4, x), 0, 1).start()

    column = lax.broadcasted_iota(jnp.int32, (8, 256), 1)
    block_row = jnp.where(column < 128, first, second)
    blocks[...] = block_row
    place = block_row[0:1] * 128 + column[0:1] % 128
    for f, block in enumerate((first, second)):
        key_place = block * 128 + lax.broadcasted_iota(jnp.int32, (128, 256), 0)
        diag[128 * f : 128 * f + 128, :] = jnp.where(key_place <= place, 0.0, -BIG)

    loads[3].wait()
    for load in loads[4:]:
        load.start()
    zero = jnp.zeros((64, 256), jnp.bfloat16)
    for half in range(2):
        q = jnp.dot(
            normed[...], wq[:, 256 * half : 256 * half + 256], preferred_element_type=jnp.float32
        ).T
        for n in range(4):
            u = (rotated(q[64 * n : 64 * n + 64]) * (HD**-0.5 * LOG2E)).astype(jnp.bfloat16)
            top, low = (u, zero) if half == 0 else (zero, u)
            qp[half, n, 0:64, :] = top
            qp[half, n, 64:128, :] = low

    def weigh(row, ja, jb, first):
        g, n = row // 4, row % 4
        pa = jnp.exp2(s_ref[row, 0:128, :] - mo_ref[0, row : row + 1, :])
        pb = jnp.exp2(s_ref[row, 128:256, :] - mo_ref[1, row : row + 1, :])
        p = jnp.concatenate([pa, pb], axis=0).astype(jnp.bfloat16)
        va = kv[ja, 128 + 64 * g : 192 + 64 * g, :]
        vb = kv[jb, 128 + 64 * g : 192 + 64 * g, :]
        vt = jnp.concatenate([jnp.concatenate([va, vb], axis=1), jnp.ones((16, 256), jnp.bfloat16)], axis=0)
        o = jnp.dot(vt, p, preferred_element_type=jnp.float32)
        total, o = o[64:65], o[0:64]
        if first:
            l_ref[row : row + 1, :] = total
            acc[64 * row : 64 * row + 64, :] = o
        else:
            factor = f_ref[row : row + 1, :]
            l_ref[row : row + 1, :] = l_ref[row : row + 1, :] * factor + total
            acc[64 * row : 64 * row + 64, :] = acc[64 * row : 64 * row + 64, :] * factor + o

    def score(row, ja, jb, first):
        g, n = row // 4, row % 4
        sa = jnp.dot(kv[ja, 0:128, :], qp[g, n], preferred_element_type=jnp.float32)
        sb = jnp.dot(kv[jb, 0:128, :], qp[g, n], preferred_element_type=jnp.float32)
        if first:
            sa = sa + diag[0:128, :]
            sb = sb + diag[128:256, :]
        s_ref[row, 0:128, :] = sa
        s_ref[row, 128:256, :] = sb
        ma, mb = jnp.max(sa, axis=0, keepdims=True), jnp.max(sb, axis=0, keepdims=True)
        if first:
            new = jnp.maximum(ma, mb)
            mo_ref[0, row : row + 1, :] = new
            mo_ref[1, row : row + 1, :] = new
        else:
            ba = jnp.where(blocks[0:1, :] < order[ja], BIG, 0.0)
            bb = jnp.where(blocks[0:1, :] < order[jb], BIG, 0.0)
            old = m_ref[row : row + 1, :]
            new = jnp.maximum(old, jnp.maximum(ma - ba, mb - bb))
            f_ref[row : row + 1, :] = jnp.exp2(old - new)
            mo_ref[0, row : row + 1, :] = new + ba
            mo_ref[1, row : row + 1, :] = new + bb
        m_ref[row : row + 1, :] = new

    def attend(before, now):
        for row in range(8):
            weigh(row, *before, False)
            score(row, *now, False)
        return now

    for row in range(8):
        score(row, 2 * b, 2 * b + 1, True)
    for row in range(8):
        l_ref[row : row + 1, :] = jnp.zeros((1, 256), jnp.float32)
        acc[64 * row : 64 * row + 64, :] = jnp.zeros((64, 256), jnp.float32)
        f_ref[row : row + 1, :] = jnp.zeros((1, 256), jnp.float32)
    held = (2 * b, 2 * b + 1)

    def source(f, i, ds):
        major, minor = coords[f]
        pp, xx = plane(i, major, x)
        return origin(f, pp, (minor + ds) % 4, xx)

    def take_plane(i):
        for f in range(2):
            major, minor = coords[f]
            org = source(f, i, 0)
            arrived(f, org)

            @pl.when((i == 1) | (i == 2))
            def _():
                copy(f, org, origin(f, (major + 1) % 4, minor, x), i, 2).start()

            @pl.when((i == 1) | (i == 5))
            def _():
                copy(f, org, origin(f, (major + 3) % 4, minor, x), i, 3).start()

            copy(f, org, origin(f, major, (minor + 1) % 4, x), i, 0).start()
            copy(f, org, origin(f, major, (minor + 3) % 4, x), i, 1).start()

    def take_near(i, back, passing=False):
        for f in range(2):
            major, minor = coords[f]
            org = source(f, i, 1 + 2 * back)
            arrived(f, org)

            if passing:

                @pl.when((i // 2) % 2 == 1 - back)
                def _():
                    copy(f, org, origin(f, major, (minor + 3 + 2 * back) % 4, x), i, 5).start()

    def take_far(i, passing=False):
        for f in range(2):
            org = source(f, i, 2)
            arrived(f, org)
            if passing:
                copy(f, org, origin(f, *coords[f], (x + 1) % 2), i + 1, 5).start()

    def step(held, i, ds):
        return attend(held, (2 * source(0, i, ds), 2 * source(1, i, ds) + 1))

    def plane_even(k, held):
        take_plane(2 * k)
        return step(held, 2 * k, 0)

    def near_even(n, held):
        take_near(n // 2 * 2, (n + 1) % 2, True)

        @pl.when((n == 1) | (n == 2))
        def _():
            take_plane(5 * n - 4)

        @pl.when((n == 6) | (n == 7))
        def _():
            take_plane(2 * n - 9)

        return step(held, n // 2 * 2, 1 + 2 * ((n + 1) % 2))

    def far_even(k, held):
        take_far(2 * k, True)

        @pl.when(k == 2)
        def _():
            take_near(1, 1)
            take_near(1, 0)

        return step(held, 2 * k, 2)

    def plane_odd(k, held):
        @pl.when(k == 0)
        def _():
            take_plane(7)

        @pl.when((k == 1) | (k == 3))
        def _():
            take_near(k + 2, 1)
            take_near(k + 2, 0)

        return step(held, 2 * k + 1, 0)

    def near_odd(n, held):
        @pl.when(n == 2)
        def _():
            take_near(7, 1)
            take_near(7, 0)

        return step(held, n // 2 * 2 + 1, 1 + 2 * ((n + 1) % 2))

    def far_odd(k, held):
        take_far(2 * k + 1)
        return step(held, 2 * k + 1, 2)

    held = lax.fori_loop(1, 3, plane_even, held)
    held = lax.fori_loop(0, 8, near_even, held)
    held = step(held, 6, 0)
    held = lax.fori_loop(0, 4, far_even, held)
    held = lax.fori_loop(0, 4, plane_odd, held)
    held = lax.fori_loop(0, 8, near_odd, held)
    held = lax.fori_loop(0, 4, far_odd, held)
    for row in range(8):
        weigh(row, *held, False)

    for n in range(8):
        inv = 1.0 / l_ref[n : n + 1, :]
        heads[:, 64 * n : 64 * n + 64] = (acc[64 * n : 64 * n + 64, :] * inv).T.astype(jnp.bfloat16)

    def sent(i, _):
        for f in range(2):
            for which in (0, 1, 5):
                copy(f, b, peers[0], i, which).wait_send()
        return 0

    lax.fori_loop(0, 8, sent, 0)
    for f in range(2):
        for i, which in ((0, 4), (0, 2), (0, 3), (1, 2), (1, 3), (2, 2), (5, 3)):
            copy(f, b, peers[0], i, which).wait_send()

    def tail_copy(stage, r, src, dst, peer):
        return pltpu.make_async_remote_copy(
            src_ref=src, dst_ref=dst,
            send_sem=tail_send.at[stage, r], recv_sem=tail_recv.at[stage, r],
            device_id={"tp": peer}, device_id_type=MESH,
        )

    def columns(c):
        return pl.ds(pl.multiple_of(c * SHARE, SHARE), SHARE)

    def rows_of(q):
        return slice(PIECE * q, PIECE * q + PIECE)

    def chunk_rows(r):
        return slice(ROWS * r, ROWS * r + ROWS)

    def near_copy(stage, q, j):
        at = rows_of(q)
        return tail_copy(
            (0, 2, 7, 8)[2 * j + stage], q, near_out.at[stage, j, at], near_in.at[stage, j, at], twin
        )

    def far_copy(stage, q):
        return tail_copy(
            2 * stage + 1, q, far_out.at[stage, rows_of(q)], far_in.at[stage, rows_of(q)], across
        )

    def give(stage, pieces, j, lhs, w):
        at = slice(PIECE * pieces[0], PIECE * pieces[-1] + PIECE)
        part = jnp.dot(lhs[at, :], w[:, columns((twin + 2 - 2 * j) % 4)], preferred_element_type=jnp.float32)
        near_out[stage, j, at] = part.astype(jnp.bfloat16)
        for q in pieces:
            near_copy(stage, q, j).start()

    def keep(pieces, j, lhs, w):
        at = slice(PIECE * pieces[0], PIECE * pieces[-1] + PIECE)
        kept[j, at] = jnp.dot(lhs[at, :], w[:, columns((across, t)[j])], preferred_element_type=jnp.float32)

    def cross(stage, q):
        at = rows_of(q)
        near_copy(stage, q, 0).wait()
        far_out[stage, at] = (kept[0, at] + near_in[stage, 0, at].astype(jnp.float32)).astype(jnp.bfloat16)
        far_copy(stage, q).start()

    def total(stage, q):
        at = rows_of(q)
        near_copy(stage, q, 1).wait()
        far_copy(stage, q).wait()
        return kept[1, at] + near_in[stage, 1, at].astype(jnp.float32) + far_in[stage, at].astype(jnp.float32)

    def share_copy(stage, q, slot, peer):
        return tail_copy(stage, q, shares.at[q, slot], shares.at[q, slot], peer)

    def chip_rows(chip):
        return pl.ds(pl.multiple_of(chip * 2 * SHARE, 2 * SHARE), 2 * SHARE)

    def norm_part(q, c, add):
        u = shares[q, c].astype(jnp.float32)
        square = jnp.sum(u * u, axis=-1, keepdims=True)
        squares[rows_of(q), :] = squares[rows_of(q), :] + square if add else jnp.broadcast_to(square, (PIECE, 128))
        normed[rows_of(q), columns(c)] = (u * gain2[:, columns(c)]).astype(jnp.bfloat16)

    here = t // 2
    every = range(256 // PIECE)
    loads[4].wait()
    give(0, every, 0, heads, wo)
    keep(every, 0, heads, wo)
    give(0, every, 1, heads, wo)
    for q in every:
        cross(0, q)
    keep(every, 1, heads, wo)

    def share_out(q):
        own = tok[rows_of(q), columns(t)].astype(jnp.float32) + total(0, q)
        resid[rows_of(q), :] = own
        shares[q, t] = own.astype(jnp.bfloat16)
        share_copy(4, q, t, across).start()
        share_copy(5, q, t, twin).start()

    def pieces_of(r):
        return range(ROWS // PIECE * r, ROWS // PIECE * (r + 1))

    def half_units(r):
        for q in pieces_of(r):
            norm_part(q, t, False)
        for q in pieces_of(r):
            share_copy(5, q, twin, twin).wait_recv()
            norm_part(q, twin, True)

        def units(n, _):
            at = pl.ds(pl.multiple_of(n * UNITS, UNITS), UNITS)
            u = normed[chunk_rows(r), chip_rows(here)]
            gated[r, 0, :, at] = jnp.dot(u, wg[chip_rows(here), at], preferred_element_type=jnp.float32)
            gated[r, 1, :, at] = jnp.dot(u, wu[chip_rows(here), at], preferred_element_type=jnp.float32)
            return 0

        lax.fori_loop(0, 2048 // UNITS, units, 0)

    def pass_on(q):
        share_copy(4, q, across, across).wait_recv()
        share_copy(6, q, across, twin).start()

    def other_units(r):
        for q in pieces_of(r):
            norm_part(q, across, True)
        for q in pieces_of(r):
            share_copy(6, q, (twin + 2) % 4, twin).wait_recv()
            norm_part(q, (twin + 2) % 4, True)
        scale = lax.rsqrt(squares[chunk_rows(r), 0:1] * (1.0 / (4 * SHARE)) + EPS)

        def units(n, _):
            at = pl.ds(pl.multiple_of(n * UNITS, UNITS), UNITS)
            u = normed[chunk_rows(r), chip_rows(1 - here)]
            gate = jnp.dot(u, wg[chip_rows(1 - here), at], preferred_element_type=jnp.float32)
            up = jnp.dot(u, wu[chip_rows(1 - here), at], preferred_element_type=jnp.float32)
            gate = (gate + gated[r, 0, :, at]) * scale
            up = (up + gated[r, 1, :, at]) * scale
            hidden[chunk_rows(r), at] = (gate / (1.0 + jnp.exp(-gate)) * up).astype(jnp.bfloat16)
            return 0

        lax.fori_loop(0, 2048 // UNITS, units, 0)

    def down(r):
        pieces = pieces_of(r)
        give(1, pieces, 0, hidden, wd)
        keep(pieces, 0, hidden, wd)
        give(1, pieces, 1, hidden, wd)
        for q in pieces:
            cross(1, q)
        keep(pieces, 1, hidden, wd)

    share_out(0)
    share_out(1)
    loads[5].wait()
    loads[6].wait()
    half_units(0)
    share_out(2)
    share_out(3)
    pass_on(0)
    half_units(1)
    pass_on(1)
    loads[7].wait()
    other_units(0)
    pass_on(2)
    pass_on(3)
    down(0)
    other_units(1)
    down(1)
    for q in every:
        out[rows_of(q), :] = (resid[rows_of(q), :] + total(1, q)).astype(jnp.bfloat16)
    for q in every:
        share_copy(4, q, t, across).wait_send()
        share_copy(5, q, t, twin).wait_send()
        share_copy(6, q, across, twin).wait_send()


def layer(tok, order, gain, wq, wk, wv, tab, gain2, wo, wg, wu, wd):
    vmem = pl.BlockSpec(memory_space=pltpu.VMEM)
    hbm = pl.BlockSpec(memory_space=pl.ANY)
    bf16, f32 = jnp.bfloat16, jnp.float32
    return pl.pallas_call(
        layer_kernel,
        out_shape=jax.ShapeDtypeStruct((256, SHARE), bf16),
        in_specs=[hbm, pl.BlockSpec(memory_space=pltpu.SMEM), vmem, hbm, hbm, hbm, vmem, vmem, hbm, hbm, hbm, hbm],
        out_specs=vmem,
        scratch_shapes=[
            pltpu.VMEM((256, 256), f32),
            pltpu.VMEM((8, 256), jnp.int32),
            pltpu.VMEM((CHUNKS, 2, ROWS, 2048), f32),
            pltpu.VMEM((256, 128), f32),
            pltpu.VMEM((256, 2048), bf16),
            pltpu.VMEM((2048, 512), bf16),
            pltpu.VMEM((2048, 128), bf16),
            pltpu.VMEM((2048, 128), bf16),
            pltpu.VMEM((512, 2048), bf16),
            pltpu.VMEM((2048, 2048), bf16),
            pltpu.VMEM((2048, 2048), bf16),
            pltpu.VMEM((2048, 2048), bf16),
            pltpu.VMEM((256, 512), bf16),
            pltpu.VMEM((2, 2, 256, SHARE), bf16),
            pltpu.VMEM((2, 2, 256, SHARE), bf16),
            pltpu.VMEM((2, 256, SHARE), bf16),
            pltpu.VMEM((2, 256, SHARE), bf16),
            pltpu.VMEM((2, 256, SHARE), f32),
            pltpu.VMEM((256, SHARE), f32),
            pltpu.VMEM((256 // PIECE, 4, PIECE, SHARE), bf16),
            pltpu.VMEM((256, 2048), bf16),
            pltpu.SemaphoreType.DMA((8,)),
            pltpu.SemaphoreType.DMA((9, 256 // PIECE)),
            pltpu.SemaphoreType.DMA((9, 256 // PIECE)),
            pltpu.VMEM((256, 2048), bf16),
            pltpu.VMEM((64, 256, 128), bf16),
            pltpu.VMEM((2, 4, 128, 256), bf16),
            pltpu.VMEM((8, 256, 256), f32),
            pltpu.VMEM((2, 8, 256), f32),
            pltpu.VMEM((8, 256), f32),
            pltpu.VMEM((8, 256), f32),
            pltpu.VMEM((8, 256), f32),
            pltpu.VMEM((512, 256), f32),
            pltpu.SemaphoreType.DMA((2, 8, 6)),
            pltpu.SemaphoreType.DMA((64,)),
        ],
        compiler_params=pltpu.CompilerParams(
            collective_id=0, has_side_effects=True, vmem_limit_bytes=62 * 1024 * 1024
        ),
        name="layer",
    )(tok, order, gain, wq, wk, wv, tab, gain2, wo, wg, wu, wd)


def local(tokens, order, gain_attn, gain_ffn, w_query, w_key, w_value, w_out, w_gate, w_up, w_down):
    return layer(
        tokens, order, gain_attn[None, :], w_query, w_key, w_value, jnp.asarray(rope_table()),
        gain_ffn[None, :], w_out, w_gate, w_up, w_down,
    )


def solution(mesh):
    placed = (
        P("blk", None),
        P(),
        P(),
        P(),
        P(None, "tp"),
        P(None, "tp"),
        P(None, "tp"),
        P("tp", None),
        P(None, "tp"),
        P(None, "tp"),
        P("tp", None),
    )
    return jax.shard_map(
        local, mesh=mesh, in_specs=placed, out_specs=P("blk", "tp"), check_vma=False
    )
```

time: 82.8 us -> 72.2 us (0.87)
  Pallas kernels: 76.9 us -> 70.4 us
  other arithmetic: 3.08 us -> 0 us
    pallas_call x1, Pallas kernels: 76.9 us -> 70.4 us  [layer(): pl.pallas_call(layer_kernel, out_shape=jax.ShapeDtypeStruct((256, SHARE),...]
    select_n x2 -> x0, other arithmetic: 2.16 us -> none  [the longest x1 1.36 us: local(): jnp.where(order[:, None] > block_of[None, :], BIG, 0.0).astype(jnp.float32)]
    sin x1 -> x0, other arithmetic: 0.83 us -> none  [local(): jnp.sin(angle)]
where the time goes in v3:
time: 72.2 us; the launch traced here: 72.1 us
  Pallas kernels  70.4 us (98%)
  local copies, waits for them, and re-layouts  1.67 us (2%)
    pallas_call x1, Pallas kernels, layer(): pl.pallas_call(layer_kernel, out_shape=jax.ShapeDtypeStruct((256, SHARE),...  70.4 us
    unnamed x1, local copies, waits for them, and re-layouts  1.67 us

profile of v3, /device:TPU:1, one launch (start us, length us, event | category | flops | bytes accessed | tf_op | source)
XLA Modules:
  0.0 72.1 jit_solution(5665289980578208862)
XLA Ops:
  0.0 70.4 %layer.1 = bf16[256,512]{1,0:T(8,128)(2,1)} custom-call(bf16[256,2048]{1,0:T(8,128)(2,1)} %tok_hbm.1, s32[64]{0:T(128)} %order.1, f32[1,2048]{1,0:T(1,128)} %bitcast.2, bf16[2048,512]{1,0:T(8,128)(2,1)} %wq_hbm.1, bf16[2048,128]{1,0:T(8,128)(2,1)} %wk_hbm.1, bf16[2048,128]{1,0:T(8,128)(2,1)} %wv_hbm.1, f32[128,128]{1,0:T(8,128)} %constant.2.clone.tab, ...), custom_call_target="tpu_custom_call" | custom-call | tf_op jit(solution)/shard_map/layer/pallas_call | solution.py:497
  70.4 1.7 %copy.14 = bf16[256,512]{1,0:T(8,128)(2,1)} copy(bf16[256,512]{1,0:T(8,128)(2,1)} %layer.1) | data formatting | bytes 524288

commit v4 on v3

--- a/solution.py
+++ b/solution.py
@@ -17,6 +17,49 @@
 BIG = 1e30
 LOG2E = 1.4426950408889634
 MESH = pl.DeviceIdType.MESH
+
+
+ORDER = (
+    (2, 0), (4, 0), (0, 3), (0, 1), (1, 0), (2, 1), (6, 0), (2, 3),
+    (4, 1), (4, 3), (5, 0), (1, 3), (0, 2), (6, 1), (2, 2), (3, 0),
+    (1, 1), (6, 3), (7, 0), (5, 3), (5, 1), (3, 1), (4, 2), (6, 2),
+    (1, 2), (7, 1), (3, 3), (7, 3), (3, 2), (5, 2), (7, 2),
+)
+EVENTS = (
+    ((2, 0), (4, 0)),
+    (),
+    ((0, 3), (0, 1)),
+    (),
+    ((1, 0),),
+    ((6, 0), (2, 1)),
+    (),
+    ((2, 3), (4, 1)),
+    (),
+    ((5, 0), (4, 3)),
+    (),
+    ((1, 3),),
+    ((6, 1), (0, 2)),
+    (),
+    ((3, 0), (2, 2)),
+    (),
+    ((1, 1),),
+    ((7, 0), (6, 3)),
+    (),
+    ((5, 3), (5, 1)),
+    (),
+    ((3, 1),),
+    ((4, 2), (6, 2)),
+    (),
+    ((1, 2), (7, 1)),
+    (),
+    ((3, 3),),
+    ((7, 3),),
+    ((3, 2),),
+    ((5, 2),),
+    ((7, 2),),
+    (),
+)
+CODES = [sum((4 * i + ds) << (5 * j) for j, (i, ds) in enumerate(ORDER[p : p + 6])) for p in range(0, 31, 6)]
 
 
 def rope_table():
@@ -219,103 +262,46 @@
         pp, xx = plane(i, major, x)
         return origin(f, pp, (minor + ds) % 4, xx)
 
-    def take_plane(i):
+    def take(i, ds):
         for f in range(2):
             major, minor = coords[f]
-            org = source(f, i, 0)
+            org = source(f, i, ds)
             arrived(f, org)
-
-            @pl.when((i == 1) | (i == 2))
+            if ds == 0:
+                if i in (1, 2):
+                    copy(f, org, origin(f, (major + 1) % 4, minor, x), i, 2).start()
+                if i in (1, 5):
+                    copy(f, org, origin(f, (major + 3) % 4, minor, x), i, 3).start()
+                if i not in (1, 3):
+                    copy(f, org, origin(f, major, (minor + 1) % 4, x), i, 0).start()
+                    copy(f, org, origin(f, major, (minor + 3) % 4, x), i, 1).start()
+            elif ds != 2:
+                if i in (0, 2):
+                    copy(f, org, origin(f, major, minor, (x + 1) % 2), i + 1, ds // 3).start()
+                if (i // 2) % 2 == (ds == 1):
+                    copy(f, org, origin(f, major, (minor + 4 - ds) % 4, x), i, 5).start()
+
+    def one_step(n, held):
+        for group in range(0, 32, 8):
+
+            @pl.when(n // 8 == group // 8)
             def _():
-                copy(f, org, origin(f, (major + 1) % 4, minor, x), i, 2).start()
-
-            @pl.when((i == 1) | (i == 5))
-            def _():
-                copy(f, org, origin(f, (major + 3) % 4, minor, x), i, 3).start()
-
-            copy(f, org, origin(f, major, (minor + 1) % 4, x), i, 0).start()
-            copy(f, org, origin(f, major, (minor + 3) % 4, x), i, 1).start()
-
-    def take_near(i, back, passing=False):
-        for f in range(2):
-            major, minor = coords[f]
-            org = source(f, i, 1 + 2 * back)
-            arrived(f, org)
-
-            if passing:
-
-                @pl.when((i // 2) % 2 == 1 - back)
-                def _():
-                    copy(f, org, origin(f, major, (minor + 3 + 2 * back) % 4, x), i, 5).start()
-
-    def take_far(i, passing=False):
-        for f in range(2):
-            org = source(f, i, 2)
-            arrived(f, org)
-            if passing:
-                copy(f, org, origin(f, *coords[f], (x + 1) % 2), i + 1, 5).start()
-
-    def step(held, i, ds):
+                for at in range(group, group + 8):
+                    if EVENTS[at]:
+
+                        @pl.when(n == at)
+                        def _():
+                            for i, ds in EVENTS[at]:
+                                take(i, ds)
+
+        code = jnp.int32(CODES[-1])
+        for part in range(len(CODES) - 2, -1, -1):
+            code = jnp.where(n < 6 * part + 6, CODES[part], code)
+        code = lax.shift_right_logical(code, 5 * (n % 6)) % 32
+        i, ds = code // 4, code % 4
         return attend(held, (2 * source(0, i, ds), 2 * source(1, i, ds) + 1))
 
-    def plane_even(k, held):
-        take_plane(2 * k)
-        return step(held, 2 * k, 0)
-
-    def near_even(n, held):
-        take_near(n // 2 * 2, (n + 1) % 2, True)
-
-        @pl.when((n == 1) | (n == 2))
-        def _():
-            take_plane(5 * n - 4)
-
-        @pl.when((n == 6) | (n == 7))
-        def _():
-            take_plane(2 * n - 9)
-
-        return step(held, n // 2 * 2, 1 + 2 * ((n + 1) % 2))
-
-    def far_even(k, held):
-        take_far(2 * k, True)
-
-        @pl.when(k == 2)
-        def _():
-            take_near(1, 1)
-            take_near(1, 0)
-
-        return step(held, 2 * k, 2)
-
-    def plane_odd(k, held):
-        @pl.when(k == 0)
-        def _():
-            take_plane(7)
-
-        @pl.when((k == 1) | (k == 3))
-        def _():
-            take_near(k + 2, 1)
-            take_near(k + 2, 0)
-
-        return step(held, 2 * k + 1, 0)
-
-    def near_odd(n, held):
-        @pl.when(n == 2)
-        def _():
-            take_near(7, 1)
-            take_near(7, 0)
-
-        return step(held, n // 2 * 2 + 1, 1 + 2 * ((n + 1) % 2))
-
-    def far_odd(k, held):
-        take_far(2 * k + 1)
-        return step(held, 2 * k + 1, 2)
-
-    held = lax.fori_loop(1, 3, plane_even, held)
-    held = lax.fori_loop(0, 8, near_even, held)
-    held = step(held, 6, 0)
-    held = lax.fori_loop(0, 4, far_even, held)
-    held = lax.fori_loop(0, 4, plane_odd, held)
-    held = lax.fori_loop(0, 8, near_odd, held)
-    held = lax.fori_loop(0, 4, far_odd, held)
+    held = lax.fori_loop(0, 31, one_step, held)
     for row in range(8):
         weigh(row, *held, False)
 

time: 72.2 us -> 70.1 us (0.971)
  Pallas kernels: 70.4 us -> 68.2 us
    pallas_call x1, Pallas kernels: 70.4 us -> 68.2 us  [layer(): pl.pallas_call(layer_kernel, out_shape=jax.ShapeDtypeStruct((256, SHARE),...]
where the time goes in v4:
time: 70.1 us; the launch traced here: 69.9 us
  Pallas kernels  68.2 us (97%)
  local copies, waits for them, and re-layouts  1.67 us (2%)
    pallas_call x1, Pallas kernels, layer(): pl.pallas_call(layer_kernel, out_shape=jax.ShapeDtypeStruct((256, SHARE),...  68.2 us
    unnamed x1, local copies, waits for them, and re-layouts  1.67 us

profile of v4, /device:TPU:1, one launch (start us, length us, event | category | flops | bytes accessed | tf_op | source)
XLA Modules:
  0.0 69.9 jit_solution(16311120120929336389)
XLA Ops:
  0.0 68.2 %layer.1 = bf16[256,512]{1,0:T(8,128)(2,1)} custom-call(bf16[256,2048]{1,0:T(8,128)(2,1)} %tok_hbm.1, s32[64]{0:T(128)} %order.1, f32[1,2048]{1,0:T(1,128)} %bitcast.2, bf16[2048,512]{1,0:T(8,128)(2,1)} %wq_hbm.1, bf16[2048,128]{1,0:T(8,128)(2,1)} %wk_hbm.1, bf16[2048,128]{1,0:T(8,128)(2,1)} %wv_hbm.1, f32[128,128]{1,0:T(8,128)} %constant.2.clone.tab, ...), custom_call_target="tpu_custom_call" | custom-call | tf_op jit(solution)/shard_map/layer/pallas_call | solution.py:483
  68.2 1.7 %copy.14 = bf16[256,512]{1,0:T(8,128)(2,1)} copy(bf16[256,512]{1,0:T(8,128)(2,1)} %layer.1) | data formatting | bytes 524288

commit v5 on v4

--- a/solution.py
+++ b/solution.py
@@ -97,11 +97,17 @@
     loads = [
         pltpu.make_async_copy(src, dst, load_sem.at[i])
         for i, (src, dst) in enumerate(
-            ((tok_hbm, tok), (wk_hbm, wk), (wv_hbm, wv), (wq_hbm, wq))
+            ((tok_hbm.at[0:64], tok.at[0:64]), (wk_hbm, wk), (wv_hbm, wv), (wq_hbm, wq))
             + ((wo_hbm, wo), (wg_hbm, wg), (wu_hbm, wu), (wd_hbm, wd))
         )
     ]
-    for load in loads[:4]:
+    more = [
+        pltpu.make_async_copy(
+            tok_hbm.at[64 * r : 64 * r + 64], tok.at[64 * r : 64 * r + 64], load_sem.at[7 + r]
+        )
+        for r in range(1, 4)
+    ]
+    for load in (loads[0], *more, *loads[1:4]):
         load.start()
     barrier = pltpu.get_barrier_semaphore()
     for peer in (twin, across):
@@ -112,17 +118,12 @@
     for peer in peers:
         pl.semaphore_signal(barrier, inc=1, device_id={"blk": peer}, device_id_type=MESH)
 
-    rows = 64
-    loads[0].wait()
-
-    def norm_rows(r, _):
-        at = pl.ds(pl.multiple_of(r * rows, rows), rows)
-        t = tok[at, :].astype(jnp.float32)
-        scale = lax.rsqrt(jnp.mean(t * t, axis=-1, keepdims=True) + EPS)
-        normed[at, :] = (t * scale * gain[...]).astype(jnp.bfloat16)
-        return 0
-
-    lax.fori_loop(0, 256 // rows, norm_rows, 0)
+    for r, load in enumerate((loads[0], *more)):
+        load.wait()
+        at = slice(64 * r, 64 * r + 64)
+        wide = tok[at, :].astype(jnp.float32)
+        scale = lax.rsqrt(jnp.mean(wide * wide, axis=-1, keepdims=True) + EPS)
+        normed[at, :] = (wide * scale * gain[...]).astype(jnp.bfloat16)
 
     first, second = order[2 * b], order[2 * b + 1]
     lane = lax.broadcasted_iota(jnp.int32, (32, 128), 1)
@@ -373,16 +374,12 @@
     def share_copy(stage, q, slot, peer):
         return tail_copy(stage, q, shares.at[q, slot], shares.at[q, slot], peer)
 
-    def chip_rows(chip):
-        return pl.ds(pl.multiple_of(chip * 2 * SHARE, 2 * SHARE), 2 * SHARE)
-
     def norm_part(q, c, add):
         u = shares[q, c].astype(jnp.float32)
         square = jnp.sum(u * u, axis=-1, keepdims=True)
         squares[rows_of(q), :] = squares[rows_of(q), :] + square if add else jnp.broadcast_to(square, (PIECE, 128))
         normed[rows_of(q), columns(c)] = (u * gain2[:, columns(c)]).astype(jnp.bfloat16)
 
-    here = t // 2
     every = range(256 // PIECE)
     loads[4].wait()
     give(0, every, 0, heads, wo)
@@ -402,42 +399,32 @@
     def pieces_of(r):
         return range(ROWS // PIECE * r, ROWS // PIECE * (r + 1))
 
-    def half_units(r):
-        for q in pieces_of(r):
-            norm_part(q, t, False)
-        for q in pieces_of(r):
-            share_copy(5, q, twin, twin).wait_recv()
-            norm_part(q, twin, True)
-
-        def units(n, _):
-            at = pl.ds(pl.multiple_of(n * UNITS, UNITS), UNITS)
-            u = normed[chunk_rows(r), chip_rows(here)]
-            gated[r, 0, :, at] = jnp.dot(u, wg[chip_rows(here), at], preferred_element_type=jnp.float32)
-            gated[r, 1, :, at] = jnp.dot(u, wu[chip_rows(here), at], preferred_element_type=jnp.float32)
-            return 0
-
-        lax.fori_loop(0, 2048 // UNITS, units, 0)
-
     def pass_on(q):
         share_copy(4, q, across, across).wait_recv()
         share_copy(6, q, across, twin).start()
 
-    def other_units(r):
+    def units_pass(r, c, turn):
         for q in pieces_of(r):
-            norm_part(q, across, True)
-        for q in pieces_of(r):
-            share_copy(6, q, (twin + 2) % 4, twin).wait_recv()
-            norm_part(q, (twin + 2) % 4, True)
-        scale = lax.rsqrt(squares[chunk_rows(r), 0:1] * (1.0 / (4 * SHARE)) + EPS)
+            if turn % 2:
+                share_copy(5 if turn == 1 else 6, q, c, twin).wait_recv()
+            norm_part(q, c, turn > 0)
+        if turn == 3:
+            scale = lax.rsqrt(squares[chunk_rows(r), 0:1] * (1.0 / (4 * SHARE)) + EPS)
 
         def units(n, _):
             at = pl.ds(pl.multiple_of(n * UNITS, UNITS), UNITS)
-            u = normed[chunk_rows(r), chip_rows(1 - here)]
-            gate = jnp.dot(u, wg[chip_rows(1 - here), at], preferred_element_type=jnp.float32)
-            up = jnp.dot(u, wu[chip_rows(1 - here), at], preferred_element_type=jnp.float32)
-            gate = (gate + gated[r, 0, :, at]) * scale
-            up = (up + gated[r, 1, :, at]) * scale
-            hidden[chunk_rows(r), at] = (gate / (1.0 + jnp.exp(-gate)) * up).astype(jnp.bfloat16)
+            u = normed[chunk_rows(r), columns(c)]
+            gate = jnp.dot(u, wg[columns(c), at], preferred_element_type=jnp.float32)
+            up = jnp.dot(u, wu[columns(c), at], preferred_element_type=jnp.float32)
+            if turn > 0:
+                gate = gate + gated[r, 0, :, at]
+                up = up + gated[r, 1, :, at]
+            if turn < 3:
+                gated[r, 0, :, at] = gate
+                gated[r, 1, :, at] = up
+            else:
+                gate, up = gate * scale, up * scale
+                hidden[chunk_rows(r), at] = (gate / (1.0 + jnp.exp(-gate)) * up).astype(jnp.bfloat16)
             return 0
 
         lax.fori_loop(0, 2048 // UNITS, units, 0)
@@ -447,26 +434,33 @@
         give(1, pieces, 0, hidden, wd)
         keep(pieces, 0, hidden, wd)
         give(1, pieces, 1, hidden, wd)
-        for q in pieces:
-            cross(1, q)
+        if r == CHUNKS - 1:
+            for q in pieces:
+                cross(1, q)
         keep(pieces, 1, hidden, wd)
 
     share_out(0)
     share_out(1)
     loads[5].wait()
     loads[6].wait()
-    half_units(0)
+    units_pass(0, t, 0)
+    units_pass(0, twin, 1)
     share_out(2)
     share_out(3)
+    units_pass(1, t, 0)
     pass_on(0)
-    half_units(1)
+    units_pass(1, twin, 1)
     pass_on(1)
     loads[7].wait()
-    other_units(0)
+    units_pass(0, across, 2)
+    units_pass(0, (twin + 2) % 4, 3)
     pass_on(2)
     pass_on(3)
     down(0)
-    other_units(1)
+    units_pass(1, across, 2)
+    cross(1, 0)
+    cross(1, 1)
+    units_pass(1, (twin + 2) % 4, 3)
     down(1)
     for q in every:
         out[rows_of(q), :] = (resid[rows_of(q), :] + total(1, q)).astype(jnp.bfloat16)
@@ -507,7 +501,7 @@
             pltpu.VMEM((256, SHARE), f32),
             pltpu.VMEM((256 // PIECE, 4, PIECE, SHARE), bf16),
             pltpu.VMEM((256, 2048), bf16),
-            pltpu.SemaphoreType.DMA((8,)),
+            pltpu.SemaphoreType.DMA((11,)),
             pltpu.SemaphoreType.DMA((9, 256 // PIECE)),
             pltpu.SemaphoreType.DMA((9, 256 // PIECE)),
             pltpu.VMEM((256, 2048), bf16),

time: 70.1 us -> 70 us (level)
  no operation moved by 1% of the time
where the time goes in v5:
time: 70 us; the launch traced here: 69.8 us
  Pallas kernels  68.1 us (97%)
  local copies, waits for them, and re-layouts  1.67 us (2%)
    pallas_call x1, Pallas kernels, layer(): pl.pallas_call(layer_kernel, out_shape=jax.ShapeDtypeStruct((256, SHARE),...  68.1 us
    unnamed x1, local copies, waits for them, and re-layouts  1.67 us

profile of v5, /device:TPU:1, one launch (start us, length us, event | category | flops | bytes accessed | tf_op | source)
XLA Modules:
  0.0 69.8 jit_solution(13042306765653869512)
XLA Ops:
  0.0 68.1 %layer.1 = bf16[256,512]{1,0:T(8,128)(2,1)} custom-call(bf16[256,2048]{1,0:T(8,128)(2,1)} %tok_hbm.1, s32[64]{0:T(128)} %order.1, f32[1,2048]{1,0:T(1,128)} %bitcast.2, bf16[2048,512]{1,0:T(8,128)(2,1)} %wq_hbm.1, bf16[2048,128]{1,0:T(8,128)(2,1)} %wk_hbm.1, bf16[2048,128]{1,0:T(8,128)(2,1)} %wv_hbm.1, f32[128,128]{1,0:T(8,128)} %constant.2.clone.tab, ...), custom_call_target="tpu_custom_call" | custom-call | tf_op jit(solution)/shard_map/layer/pallas_call | solution.py:477
  68.1 1.7 %copy.14 = bf16[256,512]{1,0:T(8,128)(2,1)} copy(bf16[256,512]{1,0:T(8,128)(2,1)} %layer.1) | data formatting | bytes 524288

commit v6 on v5

--- a/solution.py
+++ b/solution.py
@@ -21,9 +21,9 @@
 
 ORDER = (
     (2, 0), (4, 0), (0, 3), (0, 1), (1, 0), (2, 1), (6, 0), (2, 3),
-    (4, 1), (4, 3), (5, 0), (1, 3), (0, 2), (6, 1), (2, 2), (3, 0),
+    (4, 1), (4, 3), (5, 0), (1, 3), (0, 2), (6, 1), (3, 0), (2, 2),
     (1, 1), (6, 3), (7, 0), (5, 3), (5, 1), (3, 1), (4, 2), (6, 2),
-    (1, 2), (7, 1), (3, 3), (7, 3), (3, 2), (5, 2), (7, 2),
+    (1, 2), (7, 1), (3, 3), (7, 3), (5, 2), (3, 2), (7, 2),
 )
 EVENTS = (
     ((2, 0), (4, 0)),
@@ -38,24 +38,24 @@
     ((5, 0), (4, 3)),
     (),
     ((1, 3),),
-    ((6, 1), (0, 2)),
-    (),
-    ((3, 0), (2, 2)),
-    (),
+    ((0, 2),),
+    ((6, 1),),
+    ((3, 0),),
+    ((2, 2),),
     ((1, 1),),
-    ((7, 0), (6, 3)),
-    (),
-    ((5, 3), (5, 1)),
-    (),
+    ((6, 3), (7, 0)),
+    (),
+    ((5, 3),),
+    ((5, 1),),
     ((3, 1),),
     ((4, 2), (6, 2)),
     (),
-    ((1, 2), (7, 1)),
-    (),
-    ((3, 3),),
-    ((7, 3),),
+    ((1, 2),),
+    ((7, 1),),
+    ((3, 3), (7, 3)),
+    (),
+    ((5, 2),),
     ((3, 2),),
-    ((5, 2),),
     ((7, 2),),
     (),
 )

time: 70 us -> 70 us (level)
  no operation moved by 1% of the time
where the time goes in v6:
time: 70 us; the launch traced here: 69.8 us
  Pallas kernels  68.1 us (97%)
  local copies, waits for them, and re-layouts  1.67 us (2%)
    pallas_call x1, Pallas kernels, layer(): pl.pallas_call(layer_kernel, out_shape=jax.ShapeDtypeStruct((256, SHARE),...  68.1 us
    unnamed x1, local copies, waits for them, and re-layouts  1.67 us

profile of v6, /device:TPU:1, one launch (start us, length us, event | category | flops | bytes accessed | tf_op | source)
XLA Modules:
  0.0 69.8 jit_solution(4175980905601038085)
XLA Ops:
  0.0 68.1 %layer.1 = bf16[256,512]{1,0:T(8,128)(2,1)} custom-call(bf16[256,2048]{1,0:T(8,128)(2,1)} %tok_hbm.1, s32[64]{0:T(128)} %order.1, f32[1,2048]{1,0:T(1,128)} %bitcast.2, bf16[2048,512]{1,0:T(8,128)(2,1)} %wq_hbm.1, bf16[2048,128]{1,0:T(8,128)(2,1)} %wk_hbm.1, bf16[2048,128]{1,0:T(8,128)(2,1)} %wv_hbm.1, f32[128,128]{1,0:T(8,128)} %constant.2.clone.tab, ...), custom_call_target="tpu_custom_call" | custom-call | tf_op jit(solution)/shard_map/layer/pallas_call | solution.py:477
  68.2 1.7 %copy.14 = bf16[256,512]{1,0:T(8,128)(2,1)} copy(bf16[256,512]{1,0:T(8,128)(2,1)} %layer.1) | data formatting | bytes 524288
